TPU v7x, 16 devices: a 4x2x1 block of a 4x4x8 slice. The times are simulated.
16 devices in a mesh: dp: 2 (over y, z), tp: 8 (over x, core).
Axes of the slice: x: 4, y: 2, z: 1, core: 2. Of those that a mesh axis runs over, the one named last changes fastest.
The devices are a block of a 4x4x8 slice.
Arguments:
- token_ids: int32 [4, 256], P('dp'), parts along dimension 0
- emb_table: bfloat16 [2048, 3584], P('tp')
- gain_vec: bfloat16 [3584], replicated
- w_qkv: bfloat16 [3584, 36864], P(None, 'tp')
- grad_u: bfloat16 [4, 256, 36864], P('dp', None, 'tp'), parts along dimension 0
- grad_res: bfloat16 [4, 256, 3584], P('dp', 'tp'), parts along dimension 0
Outputs:
- output 1: bfloat16 [4, 256, 36864], P('dp', None, 'tp'), parts along dimension 0
- output 2: bfloat16 [4, 256, 3584], P('dp', 'tp'), parts along dimension 0
- output 3: float32 [4096, 3584], P(('dp', 'tp')), parts along dimension 0
- output 4: float32 [3584, 73728], P(None, ('dp', 'tp')), parts along dimension 1
- output 5: float32 [7168], P('dp'), parts along dimension 0
There are 2 independent parts. A program takes and returns all parts, laid end to end along the dimension named above; an argument that names none is the same for every part.
All inputs are finite; a program needn't handle non-finite values.
Results may differ from a plain program's by a relative error of at most 0.001.
Values are sent between devices in bfloat16 or wider.
A program may use at most 768 MiB of HBM per device.

v0:
```python
import functools

import jax
import jax.numpy as jnp
from jax import lax
from jax.experimental import pallas as pl
from jax.experimental.pallas import tpu as pltpu
from jax.sharding import PartitionSpec as P

NORM_EPS = 1e-6
MESH = pl.DeviceIdType.MESH
F32 = jnp.float32
BF16 = jnp.bfloat16
DN_TILE = 256
RELAY_AT = (3, 5)
SUM_AT = (10, 12)
DW_ROWS = 256
U_COLS = 512
U_HOOKS = (2, 3, 4, 5, 6, 7)
DE_COLS = 512


def gather_kernel(group, ids_ref, gain_ref, table_ref, w_ref, du_ref,
                  n_out, xchip_out, plus_out, minus_out, keep_out,
                  tab, looked, r_relay, r_direct, r_comb, s_comb, xbuf, n_v, du_v, wbuf, dn2, dnp, stage,
                  lsem, wsem, osem, snd, rcv):
    dev = lax.axis_index('tp')
    chips = group // 2
    chip = lax.div(dev, 2)
    core = lax.rem(dev, 2)
    plus = lax.rem(dev + 2, group)
    minus = lax.rem(dev + group - 2, group)
    partner = dev + 1 - 2 * core
    micro, seq_len = ids_ref.shape
    rows_loc, model_dim = table_ref.shape
    half = model_dim // 2
    ctok = seq_len // chips
    qrows = ctok // 2
    tiles = half // DN_TILE
    my_cols = pl.ds(pl.multiple_of(core * half, 128), half)
    his_cols = pl.ds(pl.multiple_of((1 - core) * half, 128), half)

    def rel(j):
        return lax.rem(chip + j, chips)

    def tok(d, q=None):
        if q is None:
            return pl.ds(pl.multiple_of(d * ctok, ctok), ctok)
        return pl.ds(pl.multiple_of(d * ctok + q * qrows, qrows), qrows)

    def remote(src, dst, slot, target):
        return pltpu.make_async_remote_copy(src_ref=src, dst_ref=dst, send_sem=snd.at[slot], recv_sem=rcv.at[slot],
                                            device_id={'tp': target}, device_id_type=MESH)

    cp_du = pltpu.make_async_copy(du_ref, du_v, lsem.at[0])
    cp_tab = pltpu.make_async_copy(table_ref.at[:, my_cols],
                                   tab.at[pl.ds(pl.multiple_of(core * rows_loc, rows_loc), rows_loc)], lsem.at[1])

    def w_copy(t):
        ft = jnp.where(t < tiles, (1 - core) * tiles + t, core * tiles + t - tiles)
        slot = lax.rem(t, 2)
        return pltpu.make_async_copy(w_ref.at[pl.ds(pl.multiple_of(ft * DN_TILE, DN_TILE), DN_TILE), :], wbuf.at[slot],
                                     wsem.at[slot])

    cp_tab.start()
    cp_du.start()
    w_copy(0).start()

    barrier = pltpu.get_barrier_semaphore()
    for target in (plus, minus, partner):
        pl.semaphore_signal(barrier, inc=1, device_id={'tp': target}, device_id_type=MESH)
    pl.semaphore_wait(barrier, 3)

    table_msg = remote(table_ref.at[:, his_cols], tab.at[pl.ds(pl.multiple_of(core * rows_loc, rows_loc), rows_loc)], 0, partner)
    table_msg.start()

    def relay(m, q):
        return remote(looked.at[m, tok(rel(2), q)], r_relay.at[m, q], 1 + 2 * m + q, minus if m == 0 else plus)

    def direct(m, q):
        return remote(looked.at[m, tok(rel(1 if m == 0 else 3), q)], r_direct.at[m, q], 5 + 2 * m + q, plus if m == 0 else minus)

    def comb(m, q):
        return remote(s_comb.at[m, q], r_comb.at[m, q], 9 + 2 * m + q, minus if m == 0 else plus)

    def spread(q, way):
        here = xbuf.at[:, tok(chip, q), my_cols]
        return remote(here, here, 13 + 3 * q + way, (plus, minus, partner)[way])

    def far(q, m):
        here = xbuf.at[m, tok(rel(3 if m == 0 else 1), q), my_cols]
        return remote(here, here, 19 + 2 * q + m, plus if m == 0 else minus)

    def near_fwd(q, side):
        here = xbuf.at[:, tok(rel(3 if side == 0 else 1), q), my_cols]
        return remote(here, here, 23 + 2 * q + side, partner)

    def far_fwd(q, m):
        here = xbuf.at[m, tok(rel(2), q), my_cols]
        return remote(here, here, 27 + 2 * q + m, partner)

    def dn_msg(t):
        cols = pl.ds(pl.multiple_of(t * DN_TILE, DN_TILE), DN_TILE)
        return remote(dn2.at[0, :, :, cols], dnp.at[:, :, cols], 31 + t, partner)

    cp_tab.wait()
    table_msg.wait_recv()
    row_id = lax.broadcasted_iota(jnp.int32, (2 * rows_loc, seq_len), 0) + chip * (2 * rows_loc)
    for m in (1, 0):
        hot = jnp.where(row_id == ids_ref[m:m + 1, :], 1.0, 0.0).astype(BF16)
        looked[m] = lax.dot_general(hot, tab[...], (((0,), (0,)), ((), ())), preferred_element_type=F32).astype(BF16)
    for q in range(2):
        for m in range(2):
            relay(m, q).start()
    for q in range(2):
        for m in range(2):
            direct(m, q).start()
    cp_du.wait()

    def relay_step(q):
        for m in range(2):
            relay(m, q).wait_recv()
            s_comb[m, q] = looked[m, tok(rel(3 if m == 0 else 1), q)] + r_relay[m, q]
            comb(m, q).start()

    def sum_step(q):
        for m in range(2):
            direct(m, q).wait_recv()
            comb(m, q).wait_recv()
            xbuf[m, tok(chip, q), my_cols] = (looked[m, tok(chip, q)] + r_direct[m, q]) + r_comb[m, q]
        for way in range(3):
            spread(q, way).start()

    def dn_step(t, carry):
        @pl.when(t + 1 < 2 * tiles)
        def _():
            w_copy(t + 1).start()

        w_copy(t).wait()
        slot = lax.rem(t, 2)
        part = lax.dot_general(du_v[...].reshape(micro * seq_len, du_v.shape[2]), wbuf[slot], (((1,), (1,)), ((), ())),
                               preferred_element_type=F32).astype(BF16).reshape(micro, seq_len, DN_TILE)
        side = lax.div(t, tiles)
        col = (t - side * tiles) * DN_TILE
        dn2[side, :, :, pl.ds(pl.multiple_of(col, DN_TILE), DN_TILE)] = part

        @pl.when(t < tiles)
        def _():
            dn_msg(t).start()

        for q in range(2):
            @pl.when(t == RELAY_AT[q])
            def _():
                relay_step(q)
        for q in range(2):
            @pl.when(t == SUM_AT[q])
            def _():
                sum_step(q)
        return carry

    lax.fori_loop(0, 2 * tiles, dn_step, 0)

    def dn_wait(t, carry):
        dn_msg(t).wait_recv()
        return carry

    lax.fori_loop(0, tiles, dn_wait, 0)

    terms = ((2, 1), (1, 0), (2, 0), (3, 1), (1, 1), (3, 0), (0, 0), (0, 1))

    def s_copy(i):
        out = (plus_out, minus_out, keep_out, keep_out)[i // 2]
        return pltpu.make_async_copy(stage.at[i], out.at[i % 2 if i < 4 else i - 4], osem.at[i])

    def s_steps():
        for i, (j, m) in enumerate(terms):
            stage[i] = dn2[1, m, tok(rel(j))].astype(F32) + dnp[m, tok(rel(j))].astype(F32)
            s_copy(i).start()

    def near_step(q):
        spread(q, 0).wait_recv()
        far(q, 0).start()
        near_fwd(q, 0).start()
        spread(q, 1).wait_recv()
        far(q, 1).start()
        near_fwd(q, 1).start()

    near_step(0)
    s_steps()
    near_step(1)

    def n_copy(d, i):
        return pltpu.make_async_copy(n_v.at[:, tok(d)], n_out.at[:, tok(d)], osem.at[2 * chips + i])

    def norm_piece(j):
        d = rel(j)

        def body(i, carry):
            m, r = lax.div(i, ctok // 16), lax.rem(i, ctok // 16)
            rows = pl.ds(pl.multiple_of(d * ctok + r * 16, 16), 16)
            xf = xbuf[m, rows].astype(F32)
            inv = lax.rsqrt(jnp.mean(xf * xf, axis=-1, keepdims=True) + NORM_EPS)
            n_v[m, rows] = (xf * inv * gain_ref[...].astype(F32)).astype(BF16)
            return carry

        lax.fori_loop(0, micro * (ctok // 16), body, 0)
        n_copy(d, j).start()

    for q in range(2):
        spread(q, 2).wait_recv()
    cp_x = pltpu.make_async_copy(xbuf.at[:, tok(chip)], xchip_out, lsem.at[0])
    cp_x.start()
    norm_piece(0)
    for q in range(2):
        for m in range(2):
            far(q, m).wait_recv()
            far_fwd(q, m).start()
    for side, j in ((0, 3), (1, 1)):
        for q in range(2):
            near_fwd(q, side).wait_recv()
        norm_piece(j)
    for q in range(2):
        for m in range(2):
            far_fwd(q, m).wait_recv()
    norm_piece(2)

    for i in range(2 * chips):
        s_copy(i).wait()
    for j in range(chips):
        n_copy(rel(j), j).wait()
    cp_x.wait()
    table_msg.wait_send()
    for q in range(2):
        for m in range(2):
            relay(m, q).wait_send()
            direct(m, q).wait_send()
            comb(m, q).wait_send()
            far(q, m).wait_send()
            far_fwd(q, m).wait_send()
            near_fwd(q, m).wait_send()
        for way in range(3):
            spread(q, way).wait_send()

    def dn_drain(t, carry):
        dn_msg(t).wait_send()
        return carry

    lax.fori_loop(0, tiles, dn_drain, 0)


def gather_call(group, ids, gain2, table, w, du):
    micro, seq_len = ids.shape
    rows_loc, model_dim = table.shape
    cols_loc = w.shape[1]
    half = model_dim // 2
    chips = group // 2
    ctok = seq_len // chips
    tiles = half // DN_TILE
    any_spec = pl.BlockSpec(memory_space=pl.ANY)
    vmem_spec = pl.BlockSpec(memory_space=pltpu.VMEM)
    msg = pltpu.VMEM((2, 2, ctok // 2, half), BF16)
    total = micro * seq_len
    return pl.pallas_call(
        functools.partial(gather_kernel, group),
        out_shape=(jax.ShapeDtypeStruct((micro, seq_len, model_dim), BF16),
                   jax.ShapeDtypeStruct((micro, ctok, model_dim), BF16),
                   jax.ShapeDtypeStruct((2, ctok, half), F32),
                   jax.ShapeDtypeStruct((2, ctok, half), F32),
                   jax.ShapeDtypeStruct((4, ctok, half), F32)),
        in_specs=[vmem_spec, vmem_spec, any_spec, any_spec, any_spec],
        out_specs=(any_spec,) * 5,
        scratch_shapes=[
            pltpu.VMEM((2 * rows_loc, half), BF16),
            pltpu.VMEM((micro, seq_len, half), BF16),
            msg, msg, msg, msg,
            pltpu.VMEM((micro, seq_len, model_dim), BF16),
            pltpu.VMEM((micro, seq_len, model_dim), BF16),
            pltpu.VMEM((micro, seq_len, cols_loc), BF16),
            pltpu.VMEM((2, DN_TILE, cols_loc), BF16),
            pltpu.VMEM((2, micro, seq_len, half), BF16),
            pltpu.VMEM((micro, seq_len, half), BF16),
            pltpu.VMEM((2 * chips, ctok, half), F32),
            pltpu.SemaphoreType.DMA((2,)),
            pltpu.SemaphoreType.DMA((2,)),
            pltpu.SemaphoreType.DMA((3 * chips,)),
            pltpu.SemaphoreType.DMA((31 + tiles,)),
            pltpu.SemaphoreType.DMA((31 + tiles,)),
        ],
        compiler_params=pltpu.CompilerParams(collective_id=0, has_side_effects=True, vmem_limit_bytes=58 * 1024 * 1024),
        cost_estimate=pl.CostEstimate(flops=2 * total * cols_loc * model_dim, bytes_accessed=2 * cols_loc * model_dim, transcendentals=0),
        name="gather_dn",
    )(ids, gain2, table, w, du)


def weight_grad_kernel(n_ref, du_ref, out_ref):
    out_ref[...] = lax.dot_general(n_ref[...], du_ref[...], (((0,), (0,)), ((), ())), preferred_element_type=F32)


def weight_grad_call(n2, du2):
    total, model_dim = n2.shape
    cols = du2.shape[1]
    return pl.pallas_call(
        weight_grad_kernel,
        grid=(model_dim // DW_ROWS,),
        out_shape=jax.ShapeDtypeStruct((model_dim, cols), F32),
        in_specs=[pl.BlockSpec((total, DW_ROWS), lambda i: (0, i)), pl.BlockSpec((total, cols), lambda i: (0, 0))],
        out_specs=pl.BlockSpec((DW_ROWS, cols), lambda i: (i, 0)),
        compiler_params=pltpu.CompilerParams(dimension_semantics=("arbitrary",), vmem_limit_bytes=40 * 1024 * 1024),
        cost_estimate=pl.CostEstimate(flops=2 * total * cols * model_dim, bytes_accessed=4 * cols * model_dim, transcendentals=0),
        name="weight_grad",
    )(n2, du2)


def finish_kernel(group, ids_ref, gain_ref, rp_ref, rm_ref, keep_ref, xchip_ref, dres_ref, n_ref, w_ref,
                  u_out, de_out, dg_out,
                  rp, rm, keep, xc, dres, n_v, wbuf, ubuf, s_comb, r_comb, dn_v, dot_s, dot_r, dxbuf, dg_v, dg_r, dg_half, de_v,
                  lsem, wsem, usem, osem, snd, rcv):
    dev = lax.axis_index('tp')
    chips = group // 2
    chip = lax.div(dev, 2)
    core = lax.rem(dev, 2)
    plus = lax.rem(dev + 2, group)
    minus = lax.rem(dev + group - 2, group)
    opposite = lax.rem(dev + group // 2, group)
    partner = dev + 1 - 2 * core
    micro, seq_len = ids_ref.shape
    model_dim = gain_ref.shape[1]
    half = model_dim // 2
    ctok = seq_len // chips
    qrows = ctok // 2
    u_cols = wbuf.shape[2]
    steps = w_ref.shape[1] // u_cols
    rows_loc = de_out.shape[0]
    total = micro * seq_len
    my_cols = pl.ds(pl.multiple_of(core * half, 128), half)
    his_cols = pl.ds(pl.multiple_of((1 - core) * half, 128), half)

    def rel(j):
        return lax.rem(chip + j, chips)

    def tok(d, q=None):
        if q is None:
            return pl.ds(pl.multiple_of(d * ctok, ctok), ctok)
        return pl.ds(pl.multiple_of(d * ctok + q * qrows, qrows), qrows)

    def remote(src, dst, slot, target):
        return pltpu.make_async_remote_copy(src_ref=src, dst_ref=dst, send_sem=snd.at[slot], recv_sem=rcv.at[slot],
                                            device_id={'tp': target}, device_id_type=MESH)

    def local(src, dst, i):
        return pltpu.make_async_copy(src, dst, lsem.at[i])

    own_rows = pl.ds(pl.multiple_of(core * qrows, qrows), qrows)
    loads = [local(rp_ref, rp, 0), local(rm_ref, rm, 1), local(keep_ref, keep, 2), local(xchip_ref, xc, 3),
             local(n_ref, n_v, 4), local(dres_ref.at[:, :, my_cols], dres.at[:, own_rows], 5)]
    for cp in loads[:4]:
        cp.start()

    def w_copy(t):
        slot = lax.rem(t, 2)
        return pltpu.make_async_copy(w_ref.at[:, pl.ds(pl.multiple_of(t * u_cols, u_cols), u_cols)], wbuf.at[slot], wsem.at[slot])

    def u_copy(t):
        slot = lax.rem(t, 2)
        return pltpu.make_async_copy(ubuf.at[slot], u_out.at[:, :, pl.ds(pl.multiple_of(t * u_cols, u_cols), u_cols)], usem.at[slot])

    loads[4].start()
    loads[5].start()
    w_copy(0).start()

    barrier = pltpu.get_barrier_semaphore()
    for target in (plus, minus, partner, opposite):
        pl.semaphore_signal(barrier, inc=1, device_id={'tp': target}, device_id_type=MESH)
    pl.semaphore_wait(barrier, 4)

    dres_msg = remote(dres_ref.at[:, :, his_cols], dres.at[:, own_rows], 0, partner)
    dres_msg.start()

    def comb(m, q):
        return remote(s_comb.at[m, q], r_comb.at[m, q], 1 + 2 * m + q, minus if m == 0 else plus)

    def dot_msg(q):
        return remote(dot_s.at[q], dot_r.at[q], 5 + q, partner)

    def spread(q, way):
        here = dxbuf.at[:, tok(chip, q), my_cols]
        return remote(here, here, 7 + 3 * q + way, (plus, minus, partner)[way])

    def far(q, m):
        here = dxbuf.at[m, tok(rel(3 if m == 0 else 1), q), my_cols]
        return remote(here, here, 13 + 2 * q + m, plus if m == 0 else minus)

    def near_fwd(q, side):
        here = dxbuf.at[:, tok(rel(3 if side == 0 else 1), q), my_cols]
        return remote(here, here, 17 + 2 * q + side, partner)

    def far_fwd(q, m):
        here = dxbuf.at[m, tok(rel(2), q), my_cols]
        return remote(here, here, 21 + 2 * q + m, partner)

    def dg_msg(way):
        return remote(dg_v, dg_r.at[way], 25 + way, (plus, minus, opposite)[way])

    dg_fin = remote(dg_half.at[0], dg_half.at[1], 28, partner)

    for cp in loads[:4]:
        cp.wait()
    for q in range(2):
        rows = slice(q * qrows, (q + 1) * qrows)
        s_comb[1, q] = keep[0, rows] + rp[0, rows]
        comb(1, q).start()
        s_comb[0, q] = keep[1, rows] + rm[0, rows]
        comb(0, q).start()
    for cp in loads[4:]:
        cp.wait()
    dres_msg.wait_recv()
    gain_half = gain_ref[:, my_cols].astype(F32)

    def hat_of(m, rows):
        xf = xc[m, rows].astype(F32)
        inv = lax.rsqrt(jnp.mean(xf * xf, axis=-1, keepdims=True) + NORM_EPS)
        return xc[m, rows, my_cols].astype(F32) * inv, inv

    def dn_finish(q):
        rows = slice(q * qrows, (q + 1) * qrows)
        part = jnp.zeros((1, half), F32)
        for m in range(2):
            comb(m, q).wait_recv()
            direct = rp[1, rows] if m == 0 else rm[1, rows]
            dn = keep[2 + m, rows] + direct + r_comb[m, q]
            dn_v[m, rows] = dn
            hat, _ = hat_of(m, rows)
            prod = dn * hat
            part = part + jnp.sum(prod, axis=0, keepdims=True)
            dots = jnp.sum(prod * gain_half, axis=-1, keepdims=True)
            dot_s[q, m] = jnp.broadcast_to(dots, (qrows, 128))
        dot_msg(q).start()
        if q == 0:
            dg_v[...] = part
        else:
            dg_v[...] += part
            for way in range(3):
                dg_msg(way).start()

    def dx_finish(q):
        rows = slice(q * qrows, (q + 1) * qrows)
        dot_msg(q).wait_recv()
        for m in range(2):
            hat, inv = hat_of(m, rows)
            centre = (dot_s[q, m, :, :1] + dot_r[q, m, :, :1]) * (1.0 / model_dim)
            dx = dres[m, rows].astype(F32) + inv * (gain_half * dn_v[m, rows] - hat * centre)
            dxbuf[m, tok(chip, q), my_cols] = dx.astype(BF16)
        for way in range(3):
            spread(q, way).start()

    def near_step(q):
        spread(q, 0).wait_recv()
        far(q, 0).start()
        near_fwd(q, 0).start()
        spread(q, 1).wait_recv()
        far(q, 1).start()
        near_fwd(q, 1).start()

    def dg_step():
        for way in range(3):
            dg_msg(way).wait_recv()
        dg_half[0] = dg_v[...] + dg_r[0] + dg_r[1] + dg_r[2]
        dg_fin.start()

    hooks = ((U_HOOKS[0], lambda: dn_finish(0)), (U_HOOKS[1], lambda: dx_finish(0)), (U_HOOKS[2], lambda: dn_finish(1)),
             (U_HOOKS[3], lambda: dx_finish(1)), (U_HOOKS[4], lambda: near_step(0)), (U_HOOKS[5], dg_step))

    def u_step(t, carry):
        @pl.when(t + 1 < steps)
        def _():
            w_copy(t + 1).start()

        w_copy(t).wait()

        @pl.when(t >= 2)
        def _():
            u_copy(t - 2).wait()

        slot = lax.rem(t, 2)
        ubuf[slot] = jnp.dot(n_v[...].reshape(total, model_dim), wbuf[slot], preferred_element_type=F32).astype(BF16).reshape(micro, seq_len, u_cols)
        u_copy(t).start()
        for at, hook in hooks:
            pl.when(t == at)(hook)
        return carry

    lax.fori_loop(0, steps, u_step, 0)
    near_step(1)
    for q in range(2):
        for m in range(2):
            far(q, m).wait_recv()
            far_fwd(q, m).start()
    dg_fin.wait_recv()
    dg_copies = [pltpu.make_async_copy(dg_half.at[0], dg_out.at[:, my_cols], osem.at[0]),
                 pltpu.make_async_copy(dg_half.at[1], dg_out.at[:, his_cols], osem.at[1])]
    for cp in dg_copies:
        cp.start()
    row_id = lax.broadcasted_iota(jnp.int32, (rows_loc, seq_len), 0) + dev * rows_loc
    hot = jnp.concatenate([jnp.where(row_id == ids_ref[m:m + 1, :], 1.0, 0.0).astype(BF16) for m in range(micro)], axis=1)
    for q in range(2):
        spread(q, 2).wait_recv()
        for side in range(2):
            near_fwd(q, side).wait_recv()
            far_fwd(q, side).wait_recv()
    de_steps = model_dim // DE_COLS

    def de_copy(i):
        cols = pl.ds(pl.multiple_of(i * DE_COLS, DE_COLS), DE_COLS)
        return pltpu.make_async_copy(de_v.at[:, cols], de_out.at[:, cols], osem.at[2 + i])

    def de_step(i, carry):
        cols = pl.ds(pl.multiple_of(i * DE_COLS, DE_COLS), DE_COLS)
        de_v[:, cols] = jnp.dot(hot, dxbuf[:, :, cols].reshape(total, DE_COLS), preferred_element_type=F32)
        de_copy(i).start()
        return carry

    lax.fori_loop(0, de_steps, de_step, 0)

    for i in range(de_steps):
        de_copy(i).wait()
    for cp in dg_copies:
        cp.wait()
    u_copy(steps - 2).wait()
    u_copy(steps - 1).wait()
    dres_msg.wait_send()
    dg_fin.wait_send()
    for way in range(3):
        dg_msg(way).wait_send()
    for q in range(2):
        dot_msg(q).wait_send()
        for m in range(2):
            comb(m, q).wait_send()
            far(q, m).wait_send()
            far_fwd(q, m).wait_send()
            near_fwd(q, m).wait_send()
        for way in range(3):
            spread(q, way).wait_send()


def finish_call(group, rows_loc, ids, gain2, rp, rm, keep, xchip, dres, n3, w):
    micro, seq_len = ids.shape
    model_dim, cols_loc = w.shape
    half = model_dim // 2
    chips = group // 2
    ctok = seq_len // chips
    qrows = ctok // 2
    total = micro * seq_len
    any_spec = pl.BlockSpec(memory_space=pl.ANY)
    vmem_spec = pl.BlockSpec(memory_space=pltpu.VMEM)
    return pl.pallas_call(
        functools.partial(finish_kernel, group),
        out_shape=(jax.ShapeDtypeStruct((micro, seq_len, cols_loc), BF16),
                   jax.ShapeDtypeStruct((rows_loc, model_dim), F32),
                   jax.ShapeDtypeStruct((1, model_dim), F32)),
        in_specs=[vmem_spec, vmem_spec] + [any_spec] * 7,
        out_specs=(any_spec,) * 3,
        scratch_shapes=[
            pltpu.VMEM((2, ctok, half), F32),
            pltpu.VMEM((2, ctok, half), F32),
            pltpu.VMEM((4, ctok, half), F32),
            pltpu.VMEM((micro, ctok, model_dim), BF16),
            pltpu.VMEM((micro, ctok, half), BF16),
            pltpu.VMEM((micro, seq_len, model_dim), BF16),
            pltpu.VMEM((2, model_dim, U_COLS), BF16),
            pltpu.VMEM((2, micro, seq_len, U_COLS), BF16),
            pltpu.VMEM((2, 2, qrows, half), F32),
            pltpu.VMEM((2, 2, qrows, half), F32),
            pltpu.VMEM((micro, ctok, half), F32),
            pltpu.VMEM((2, micro, qrows, 128), F32),
            pltpu.VMEM((2, micro, qrows, 128), F32),
            pltpu.VMEM((micro, seq_len, model_dim), BF16),
            pltpu.VMEM((1, half), F32),
            pltpu.VMEM((3, 1, half), F32),
            pltpu.VMEM((2, 1, half), F32),
            pltpu.VMEM((rows_loc, model_dim), F32),
            pltpu.SemaphoreType.DMA((6,)),
            pltpu.SemaphoreType.DMA((2,)),
            pltpu.SemaphoreType.DMA((2,)),
            pltpu.SemaphoreType.DMA((2 + model_dim // DE_COLS,)),
            pltpu.SemaphoreType.DMA((29,)),
            pltpu.SemaphoreType.DMA((29,)),
        ],
        compiler_params=pltpu.CompilerParams(collective_id=1, has_side_effects=True, vmem_limit_bytes=58 * 1024 * 1024),
        cost_estimate=pl.CostEstimate(flops=2 * total * cols_loc * model_dim, bytes_accessed=2 * cols_loc * model_dim, transcendentals=0),
        name="finish_u",
    )(ids, gain2, rp, rm, keep, xchip, dres, n3, w)


def solution(mesh):
    group = mesh.shape['tp']
    plus = [(r, (r + 2) % group) for r in range(group)]
    minus = [(r, (r - 2) % group) for r in range(group)]

    def local_step(token_ids, table_loc, gain_vec, w_loc, du_loc, dres_loc):
        micro, seq_len = token_ids.shape
        model_dim, cols_loc = w_loc.shape
        own_tok = dres_loc.shape[1]
        total = micro * seq_len
        core = lax.rem(lax.axis_index('tp'), 2)
        gain2 = gain_vec.reshape(1, model_dim)
        normed, x_chip, msg_plus, msg_minus, keep = gather_call(group, token_ids, gain2, table_loc, w_loc, du_loc)
        got_plus = lax.ppermute(msg_plus, 'tp', plus)
        got_minus = lax.ppermute(msg_minus, 'tp', minus)
        grad_w = weight_grad_call(normed.reshape(total, model_dim), du_loc.reshape(total, cols_loc))
        u, grad_table, grad_gain = finish_call(group, table_loc.shape[0], token_ids, gain2, got_plus, got_minus, keep, x_chip, dres_loc, normed, w_loc)
        x_own = lax.dynamic_slice_in_dim(x_chip, core * own_tok, own_tok, axis=1)
        return u, x_own, grad_table, grad_w, grad_gain.reshape(model_dim)

    return jax.shard_map(local_step, mesh=mesh,
                         in_specs=(P('dp', None), P('tp', None), P(None), P(None, 'tp'), P('dp', None, 'tp'), P('dp', 'tp', None)),
                         out_specs=(P('dp', None, 'tp'), P('dp', 'tp', None), P(('dp', 'tp'), None), P(None, ('dp', 'tp')), P('dp')),
                         check_vma=False)
```

profile of v0, /device:TPU:112, one launch (start us, length us, event | category | flops | bytes accessed | tf_op | source)
XLA Modules:
  0.0 125.6 jit_solution(18024973278314786018)
XLA Ops:
  0.6 1.3 %reshape.22.gain_ref = bf16[1,3584]{1,0:T(2,128)(2,1)} reshape(bf16[3584]{0:T(1024)(128)(2,1)} %param.8) | data formatting | bytes 14336 | tf_op jit(solution)/shard_map/reshape | solution.py:604
  1.9 0.0 copy-start
  1.9 47.5 %gather_dn.1 = (bf16[2,256,3584]{2,1,0:T(8,128)(2,1)}, bf16[2,64,3584]{2,1,0:T(8,128)(2,1)}, f32[2,64,1792]{2,1,0:T(8,128)}, f32[2,64,1792]{2,1,0:T(8,128)}, f32[4,64,1792]{2,1,0:T(8,128)}) custom-call(s32[2,256]{1,0:T(2,128)} %ids_ref.3, bf16[1,3584]{1,0:T(2,128)(2,1)} %reshape.22.gain_ref, bf16[256,3584]{1,0:T(8,128)(2,1)} %table_ref.1, ...), custom_call_target="tpu_custom_call" | custom-call | flops 16911433728 | bytes 33030144 | tf_op jit(solution)/shard_map/gather_dn/pallas_call | solution.py:263
  49.5 1.2 collective-permute-start
  50.7 2.1 %collective-permute-start.1 = (f32[2,64,1792]{2,1,0:T(8,128)}, f32[2,64,1792]{2,1,0:T(8,128)}, u32[]{:S(2)}, u32[]{:S(2)}) collective-permute-start(f32[2,64,1792]{2,1,0:T(8,128)} %get-tuple-element.14), channel_id=1, source_target_pairs={{0,6},{1,7},{2,0},{3,1},{4,2},{5,3},{6,4},{7,5},{8,14},{9,15},{10,... | collective-permute-start | bytes 2752520 | tf_op jit(solution)/shard_map/ppermute | solution.py:607
  52.8 0.0 copy-done
  52.8 0.0 copy-start.1
  52.8 2.0 %copy-done.1 = bf16[2,256,3584]{2,1,0:T(8,128)(2,1)S(1)} copy-done((bf16[2,256,3584]{2,1,0:T(8,128)(2,1)S(1)}, bf16[2,256,3584]{2,1,0:T(8,128)(2,1)}, u32[]{:S(2)}) %copy-start.1) | copy-done | bytes 3670040
  54.8 0.0 copy-start.3
  54.8 26.9 %weight_grad.1 = f32[3584,4608]{1,0:T(8,128)} custom-call(bf16[512,3584]{1,0:T(8,128)(2,1)S(1)} %bitcast.3, bf16[512,4608]{1,0:T(8,128)(2,1)S(1)} %bitcast.2), custom_call_target="tpu_custom_call" | custom-call | flops 16911433728 | bytes 66060288 | tf_op jit(solution)/shard_map/weight_grad/pallas_call | solution.py:302
  81.7 0.0 copy-done.3
  81.7 0.8 constant_dynamic-slice_fusion
  82.5 0.0 collective-permute-done.rp_ref
  82.5 0.0 collective-permute-done.1.rm_ref
  82.5 34.9 %finish_u.1 = (bf16[2,256,4608]{2,1,0:T(8,128)(2,1)}, f32[256,3584]{1,0:T(8,128)}, f32[1,3584]{1,0:T(1,128)}) custom-call(s32[2,256]{1,0:T(2,128)} %ids_ref.3, bf16[1,3584]{1,0:T(2,128)(2,1)} %reshape.22.gain_ref, f32[2,64,1792]{2,1,0:T(8,128)} %collective-permute-done.rp_ref, f32[2,64,1792]{2,1,0:T(8,128)} %collective-permute-done.1.rm_ref, ...), custom_call_target="tpu_custom_call" | custom-call | flops 16911433728 | bytes 33030144 | tf_op jit(solution)/shard_map/finish_u/pallas_call | solution.py:554
  117.4 1.4 %reduce = f32[3584]{0:T(1024)} reduce(f32[1,3584]{1,0:T(1,128)} %get-tuple-element.20, f32[]{:T(128)} %constant.14), dimensions={0}, to_apply=%get-tuple-element.20.reduce_sub_computation | reduce | bytes 28676 | tf_op jit(solution)/shard_map/finish_u/pallas_call | solution.py:554
  118.8 0.0 copy-start.2
  118.8 5.0 %copy.13 = bf16[2,256,4608]{2,1,0:T(8,128)(2,1)} copy(bf16[2,256,4608]{2,1,0:T(8,128)(2,1)} %get-tuple-element.26) | data formatting | bytes 9437184
  123.8 0.0 copy-done.2
  123.8 1.8 %copy.14 = f32[256,3584]{1,0:T(8,128)} copy(f32[256,3584]{1,0:T(8,128)S(1)} %copy-done.2) | data formatting | bytes 7340032
Async XLA Ops:
  1.9 50.9 %copy-start = (bf16[2,256,4608]{2,1,0:T(8,128)(2,1)S(1)}, bf16[2,256,4608]{2,1,0:T(8,128)(2,1)}, u32[]{:S(2)}) copy-start(bf16[2,256,4608]{2,1,0:T(8,128)(2,1)} %du_ref.1) | copy-start | bytes 14155780
  49.5 33.0 %collective-permute-start = (f32[2,64,1792]{2,1,0:T(8,128)}, f32[2,64,1792]{2,1,0:T(8,128)}, u32[]{:S(2)}, u32[]{:S(2)}) collective-permute-start(f32[2,64,1792]{2,1,0:T(8,128)} %get-tuple-element.13), channel_id=1, source_target_pairs={{0,2},{1,3},{2,4},{3,5},{4,6},{5,7},{6,0},{7,1},{8,10},{9,11},{10,... | collective-permute-start | bytes 2752520 | tf_op jit(solution)/shard_map/ppermute | solution.py:606
  50.7 31.8 %collective-permute-start.1 = (f32[2,64,1792]{2,1,0:T(8,128)}, f32[2,64,1792]{2,1,0:T(8,128)}, u32[]{:S(2)}, u32[]{:S(2)}) collective-permute-start(f32[2,64,1792]{2,1,0:T(8,128)} %get-tuple-element.14), channel_id=1, source_target_pairs={{0,6},{1,7},{2,0},{3,1},{4,2},{5,3},{6,4},{7,5},{8,14},{9,15},{10,... | collective-permute-start | bytes 2752520 | tf_op jit(solution)/shard_map/ppermute | solution.py:607
  52.8 2.0 %copy-start.1 = (bf16[2,256,3584]{2,1,0:T(8,128)(2,1)S(1)}, bf16[2,256,3584]{2,1,0:T(8,128)(2,1)}, u32[]{:S(2)}) copy-start(bf16[2,256,3584]{2,1,0:T(8,128)(2,1)} %get-tuple-element.17.n_ref) | copy-start | bytes 11010052
  54.8 26.9 %copy-start.3 = (bf16[2,64,3584]{2,1,0:T(8,128)(2,1)S(1)}, bf16[2,64,3584]{2,1,0:T(8,128)(2,1)}, u32[]{:S(2)}) copy-start(bf16[2,64,3584]{2,1,0:T(8,128)(2,1)} %get-tuple-element.16.xchip_ref) | copy-start | bytes 2752516
  118.8 5.0 %copy-start.2 = (f32[256,3584]{1,0:T(8,128)S(1)}, f32[256,3584]{1,0:T(8,128)}, u32[]{:S(2)}) copy-start(f32[256,3584]{1,0:T(8,128)} %get-tuple-element.28) | copy-start | bytes 11010052
where the time goes:
time: 128 us; the launch traced here: 126 us
  Pallas kernels  109 us (85%)
  local copies, waits for them, and re-layouts  11 us (9%)
  starting transfers between devices  3.31 us (3%)
  other arithmetic  1.36 us (1%)
    pallas_call x1, Pallas kernels, gather_call(): pl.pallas_call(functools.partial(gather_kernel, group), out_shape=(jax.Sh...  47.5 us
    pallas_call x1, Pallas kernels, finish_call(): pl.pallas_call(functools.partial(finish_kernel, group), out_shape=(jax.Sh...  34.9 us
    pallas_call x1, Pallas kernels, weight_grad_call(): pl.pallas_call(weight_grad_kernel, grid=(model_dim // DW_ROWS,), out_shap...  26.9 us
    unnamed x10, local copies, waits for them, and re-layouts  8.86 us
  transfers between devices with their start and end apart: 2, of which 0 were waited for; matrix products, arithmetic and copies ran while one was open for 1% of the time, Pallas kernels for 21%

commit v1 on v0

--- a/solution.py
+++ b/solution.py
@@ -14,10 +14,12 @@
 DN_TILE = 256
 RELAY_AT = (3, 5)
 SUM_AT = (10, 12)
-DW_ROWS = 256
-U_COLS = 512
-U_HOOKS = (2, 3, 4, 5, 6, 7)
+DW_ROWS = 896
+DW_COLS = 1536
+U_COLS = 256
+U_HOOKS = (5, 7, 10, 12, 17, 15)
 DE_COLS = 512
+U_PARTS = 4
 
 
 def gather_kernel(group, ids_ref, gain_ref, table_ref, w_ref, du_ref,
@@ -192,6 +194,8 @@
     def n_copy(d, i):
         return pltpu.make_async_copy(n_v.at[:, tok(d)], n_out.at[:, tok(d)], osem.at[2 * chips + i])
 
+    gain_f = gain_ref[...].astype(F32).reshape(1, model_dim)
+
     def norm_piece(j):
         d = rel(j)
 
@@ -200,7 +204,7 @@
             rows = pl.ds(pl.multiple_of(d * ctok + r * 16, 16), 16)
             xf = xbuf[m, rows].astype(F32)
             inv = lax.rsqrt(jnp.mean(xf * xf, axis=-1, keepdims=True) + NORM_EPS)
-            n_v[m, rows] = (xf * inv * gain_ref[...].astype(F32)).astype(BF16)
+            n_v[m, rows] = (xf * inv * gain_f).astype(BF16)
             return carry
 
         lax.fori_loop(0, micro * (ctok // 16), body, 0)
@@ -256,7 +260,7 @@
     chips = group // 2
     ctok = seq_len // chips
     tiles = half // DN_TILE
-    any_spec = pl.BlockSpec(memory_space=pl.ANY)
+    hbm_spec = pl.BlockSpec(memory_space=pltpu.HBM)
     vmem_spec = pl.BlockSpec(memory_space=pltpu.VMEM)
     msg = pltpu.VMEM((2, 2, ctok // 2, half), BF16)
     total = micro * seq_len
@@ -267,8 +271,8 @@
                    jax.ShapeDtypeStruct((2, ctok, half), F32),
                    jax.ShapeDtypeStruct((2, ctok, half), F32),
                    jax.ShapeDtypeStruct((4, ctok, half), F32)),
-        in_specs=[vmem_spec, vmem_spec, any_spec, any_spec, any_spec],
-        out_specs=(any_spec,) * 5,
+        in_specs=[vmem_spec, vmem_spec, hbm_spec, hbm_spec, hbm_spec],
+        out_specs=(hbm_spec,) * 5,
         scratch_shapes=[
             pltpu.VMEM((2 * rows_loc, half), BF16),
             pltpu.VMEM((micro, seq_len, half), BF16),
@@ -293,7 +297,8 @@
 
 
 def weight_grad_kernel(n_ref, du_ref, out_ref):
-    out_ref[...] = lax.dot_general(n_ref[...], du_ref[...], (((0,), (0,)), ((), ())), preferred_element_type=F32)
+    cols = pl.ds(pl.multiple_of(pl.program_id(1) * DW_COLS, DW_COLS), DW_COLS)
+    out_ref[...] = lax.dot_general(n_ref[...], du_ref[:, cols], (((0,), (0,)), ((), ())), preferred_element_type=F32)
 
 
 def weight_grad_call(n2, du2):
@@ -301,19 +306,19 @@
     cols = du2.shape[1]
     return pl.pallas_call(
         weight_grad_kernel,
-        grid=(model_dim // DW_ROWS,),
+        grid=(model_dim // DW_ROWS, cols // DW_COLS),
         out_shape=jax.ShapeDtypeStruct((model_dim, cols), F32),
-        in_specs=[pl.BlockSpec((total, DW_ROWS), lambda i: (0, i)), pl.BlockSpec((total, cols), lambda i: (0, 0))],
-        out_specs=pl.BlockSpec((DW_ROWS, cols), lambda i: (i, 0)),
-        compiler_params=pltpu.CompilerParams(dimension_semantics=("arbitrary",), vmem_limit_bytes=40 * 1024 * 1024),
+        in_specs=[pl.BlockSpec((total, DW_ROWS), lambda i, j: (0, i)), pl.BlockSpec((total, cols), lambda i, j: (0, 0))],
+        out_specs=pl.BlockSpec((DW_ROWS, DW_COLS), lambda i, j: (i, j)),
+        compiler_params=pltpu.CompilerParams(dimension_semantics=("arbitrary", "arbitrary"), vmem_limit_bytes=63 * 1024 * 1024),
         cost_estimate=pl.CostEstimate(flops=2 * total * cols * model_dim, bytes_accessed=4 * cols * model_dim, transcendentals=0),
         name="weight_grad",
     )(n2, du2)
 
 
 def finish_kernel(group, ids_ref, gain_ref, rp_ref, rm_ref, keep_ref, xchip_ref, dres_ref, n_ref, w_ref,
-                  u_out, de_out, dg_out,
-                  rp, rm, keep, xc, dres, n_v, wbuf, ubuf, s_comb, r_comb, dn_v, dot_s, dot_r, dxbuf, dg_v, dg_r, dg_half, de_v,
+                  u_out, dx_out, dg_out,
+                  rp, rm, keep, xc, dres, n_v, wbuf, ubuf, s_comb, r_comb, dn_v, dot_s, dot_r, dxbuf, dg_v, dg_r, dg_half,
                   lsem, wsem, usem, osem, snd, rcv):
     dev = lax.axis_index('tp')
     chips = group // 2
@@ -324,13 +329,12 @@
     opposite = lax.rem(dev + group // 2, group)
     partner = dev + 1 - 2 * core
     micro, seq_len = ids_ref.shape
-    model_dim = gain_ref.shape[1]
+    model_dim = gain_ref.shape[0]
     half = model_dim // 2
     ctok = seq_len // chips
     qrows = ctok // 2
     u_cols = wbuf.shape[2]
     steps = w_ref.shape[1] // u_cols
-    rows_loc = de_out.shape[0]
     total = micro * seq_len
     my_cols = pl.ds(pl.multiple_of(core * half, 128), half)
     his_cols = pl.ds(pl.multiple_of((1 - core) * half, 128), half)
@@ -414,7 +418,7 @@
     for cp in loads[4:]:
         cp.wait()
     dres_msg.wait_recv()
-    gain_half = gain_ref[:, my_cols].astype(F32)
+    gain_half = gain_ref[my_cols].astype(F32).reshape(1, half)
 
     def hat_of(m, rows):
         xf = xc[m, rows].astype(F32)
@@ -499,29 +503,20 @@
                  pltpu.make_async_copy(dg_half.at[1], dg_out.at[:, his_cols], osem.at[1])]
     for cp in dg_copies:
         cp.start()
-    row_id = lax.broadcasted_iota(jnp.int32, (rows_loc, seq_len), 0) + dev * rows_loc
-    hot = jnp.concatenate([jnp.where(row_id == ids_ref[m:m + 1, :], 1.0, 0.0).astype(BF16) for m in range(micro)], axis=1)
     for q in range(2):
         spread(q, 2).wait_recv()
         for side in range(2):
             near_fwd(q, side).wait_recv()
+    near_copies = [pltpu.make_async_copy(dxbuf.at[:, tok(rel(j))], dx_out.at[:, tok(rel(j))], osem.at[2 + j]) for j in range(chips)]
+    for j in (0, 1, 3):
+        near_copies[j].start()
+    for q in range(2):
+        for side in range(2):
             far_fwd(q, side).wait_recv()
-    de_steps = model_dim // DE_COLS
-
-    def de_copy(i):
-        cols = pl.ds(pl.multiple_of(i * DE_COLS, DE_COLS), DE_COLS)
-        return pltpu.make_async_copy(de_v.at[:, cols], de_out.at[:, cols], osem.at[2 + i])
-
-    def de_step(i, carry):
-        cols = pl.ds(pl.multiple_of(i * DE_COLS, DE_COLS), DE_COLS)
-        de_v[:, cols] = jnp.dot(hot, dxbuf[:, :, cols].reshape(total, DE_COLS), preferred_element_type=F32)
-        de_copy(i).start()
-        return carry
-
-    lax.fori_loop(0, de_steps, de_step, 0)
-
-    for i in range(de_steps):
-        de_copy(i).wait()
+    near_copies[2].start()
+
+    for cp in near_copies:
+        cp.wait()
     for cp in dg_copies:
         cp.wait()
     u_copy(steps - 2).wait()
@@ -541,7 +536,7 @@
             spread(q, way).wait_send()
 
 
-def finish_call(group, rows_loc, ids, gain2, rp, rm, keep, xchip, dres, n3, w):
+def finish_call(group, ids, gain2, rp, rm, keep, xchip, dres, n3, w):
     micro, seq_len = ids.shape
     model_dim, cols_loc = w.shape
     half = model_dim // 2
@@ -549,14 +544,15 @@
     ctok = seq_len // chips
     qrows = ctok // 2
     total = micro * seq_len
+    hbm_spec = pl.BlockSpec(memory_space=pltpu.HBM)
     any_spec = pl.BlockSpec(memory_space=pl.ANY)
     vmem_spec = pl.BlockSpec(memory_space=pltpu.VMEM)
     return pl.pallas_call(
         functools.partial(finish_kernel, group),
         out_shape=(jax.ShapeDtypeStruct((micro, seq_len, cols_loc), BF16),
-                   jax.ShapeDtypeStruct((rows_loc, model_dim), F32),
+                   jax.ShapeDtypeStruct((micro, seq_len, model_dim), BF16),
                    jax.ShapeDtypeStruct((1, model_dim), F32)),
-        in_specs=[vmem_spec, vmem_spec] + [any_spec] * 7,
+        in_specs=[vmem_spec, vmem_spec] + [hbm_spec] * 7,
         out_specs=(any_spec,) * 3,
         scratch_shapes=[
             pltpu.VMEM((2, ctok, half), F32),
@@ -576,18 +572,76 @@
             pltpu.VMEM((1, half), F32),
             pltpu.VMEM((3, 1, half), F32),
             pltpu.VMEM((2, 1, half), F32),
-            pltpu.VMEM((rows_loc, model_dim), F32),
             pltpu.SemaphoreType.DMA((6,)),
             pltpu.SemaphoreType.DMA((2,)),
             pltpu.SemaphoreType.DMA((2,)),
-            pltpu.SemaphoreType.DMA((2 + model_dim // DE_COLS,)),
+            pltpu.SemaphoreType.DMA((2 + chips,)),
             pltpu.SemaphoreType.DMA((29,)),
             pltpu.SemaphoreType.DMA((29,)),
         ],
-        compiler_params=pltpu.CompilerParams(collective_id=1, has_side_effects=True, vmem_limit_bytes=58 * 1024 * 1024),
+        compiler_params=pltpu.CompilerParams(collective_id=1, has_side_effects=True, vmem_limit_bytes=30 * 1024 * 1024),
         cost_estimate=pl.CostEstimate(flops=2 * total * cols_loc * model_dim, bytes_accessed=2 * cols_loc * model_dim, transcendentals=0),
         name="finish_u",
     )(ids, gain2, rp, rm, keep, xchip, dres, n3, w)
+
+
+def epilogue_kernel(ids_ref, u_ref, dx_ref, dg_ref, u_out, de_out, dg_out, u_v, dx_v, de_v, usem, xsem):
+    dev = lax.axis_index('tp')
+    micro, seq_len = ids_ref.shape
+    rows_loc, model_dim = de_v.shape
+    steps = model_dim // DE_COLS
+    ucols = u_v.shape[2] // U_PARTS
+
+    def cols(i, n):
+        return pl.ds(i * n, n)
+
+    x_loads = [pltpu.make_async_copy(dx_ref.at[:, :, cols(i, DE_COLS)], dx_v.at[:, :, cols(i, DE_COLS)], xsem.at[i]) for i in range(steps)]
+    u_loads = [pltpu.make_async_copy(u_ref.at[:, :, cols(i, ucols)], u_v.at[:, :, cols(i, ucols)], usem.at[i]) for i in range(U_PARTS)]
+    x_loads[0].start()
+    x_loads[1].start()
+    for cp in u_loads:
+        cp.start()
+    for cp in x_loads[2:]:
+        cp.start()
+    dg_out[...] = dg_ref[0]
+    row_id = lax.broadcasted_iota(jnp.int32, (rows_loc, seq_len), 0) + dev * rows_loc
+    hot = jnp.concatenate([jnp.where(row_id == ids_ref[m:m + 1, :], 1.0, 0.0).astype(BF16) for m in range(micro)], axis=1)
+    u_stores = [pltpu.make_async_copy(u_v.at[:, :, cols(i, ucols)], u_out.at[:, :, cols(i, ucols)], usem.at[U_PARTS + i]) for i in range(U_PARTS)]
+    de_stores = [pltpu.make_async_copy(de_v.at[:, cols(i, DE_COLS)], de_out.at[:, cols(i, DE_COLS)], xsem.at[steps + i]) for i in range(steps)]
+    for i in range(steps):
+        x_loads[i].wait()
+        de_v[:, cols(i, DE_COLS)] = jnp.dot(hot, dx_v[:, :, cols(i, DE_COLS)].reshape(micro * seq_len, DE_COLS), preferred_element_type=F32)
+        de_stores[i].start()
+        if i < U_PARTS:
+            u_loads[i].wait()
+            u_stores[i].start()
+    for cp in u_stores + de_stores:
+        cp.wait()
+
+
+def epilogue_call(rows_loc, ids, u, dx, dg):
+    micro, seq_len, _ = u.shape
+    model_dim = dx.shape[2]
+    steps = model_dim // DE_COLS
+    any_spec = pl.BlockSpec(memory_space=pl.ANY)
+    vmem_spec = pl.BlockSpec(memory_space=pltpu.VMEM)
+    return pl.pallas_call(
+        epilogue_kernel,
+        out_shape=(jax.ShapeDtypeStruct(u.shape, BF16), jax.ShapeDtypeStruct((rows_loc, model_dim), F32),
+                   jax.ShapeDtypeStruct((model_dim,), F32)),
+        in_specs=[vmem_spec, any_spec, any_spec, vmem_spec],
+        out_specs=(any_spec, any_spec, vmem_spec),
+        scratch_shapes=[
+            pltpu.VMEM(u.shape, BF16),
+            pltpu.VMEM(dx.shape, BF16),
+            pltpu.VMEM((rows_loc, model_dim), F32),
+            pltpu.SemaphoreType.DMA((2 * U_PARTS,)),
+            pltpu.SemaphoreType.DMA((2 * steps,)),
+        ],
+        compiler_params=pltpu.CompilerParams(vmem_limit_bytes=22 * 1024 * 1024),
+        cost_estimate=pl.CostEstimate(flops=2 * micro * seq_len * rows_loc * model_dim, bytes_accessed=4 * rows_loc * model_dim, transcendentals=0),
+        name="epilogue",
+    )(ids, u, dx, dg)
 
 
 def solution(mesh):
@@ -601,14 +655,15 @@
         own_tok = dres_loc.shape[1]
         total = micro * seq_len
         core = lax.rem(lax.axis_index('tp'), 2)
-        gain2 = gain_vec.reshape(1, model_dim)
+        gain2 = gain_vec
         normed, x_chip, msg_plus, msg_minus, keep = gather_call(group, token_ids, gain2, table_loc, w_loc, du_loc)
         got_plus = lax.ppermute(msg_plus, 'tp', plus)
         got_minus = lax.ppermute(msg_minus, 'tp', minus)
         grad_w = weight_grad_call(normed.reshape(total, model_dim), du_loc.reshape(total, cols_loc))
-        u, grad_table, grad_gain = finish_call(group, table_loc.shape[0], token_ids, gain2, got_plus, got_minus, keep, x_chip, dres_loc, normed, w_loc)
+        u_tmp, dx_all, dg = finish_call(group, token_ids, gain2, got_plus, got_minus, keep, x_chip, dres_loc, normed, w_loc)
+        u, grad_table, grad_gain = epilogue_call(table_loc.shape[0], token_ids, u_tmp, dx_all, dg)
         x_own = lax.dynamic_slice_in_dim(x_chip, core * own_tok, own_tok, axis=1)
-        return u, x_own, grad_table, grad_w, grad_gain.reshape(model_dim)
+        return u, x_own, grad_table, grad_w, grad_gain
 
     return jax.shard_map(local_step, mesh=mesh,
                          in_specs=(P('dp', None), P('tp', None), P(None), P(None, 'tp'), P('dp', None, 'tp'), P('dp', 'tp', None)),

time: 128 us -> 130 us (1.016)
  Pallas kernels: 109 us -> 119 us
  local copies, waits for them, and re-layouts: 11 us -> 5.36 us
  other arithmetic: 1.36 us -> 0 us
    pallas_call x1 -> x2, Pallas kernels: 26.9 us -> 34 us  [the longest x1 28.9 us: weight_grad_call(): pl.pallas_call(weight_grad_kernel, grid=(model_dim // DW_ROWS, cols // DW...]
    unnamed x10 -> x12, local copies, waits for them, and re-layouts: 8.86 us -> 4.56 us
    pallas_call x1, Pallas kernels: 34.9 us -> 37.9 us  [finish_call(): pl.pallas_call(functools.partial(finish_kernel, group), out_shape=(jax.Sh...]
    pallas_call x1 -> x0, other arithmetic: 1.36 us -> none  [finish_call(): pl.pallas_call(functools.partial(finish_kernel, group), out_shape=(jax.Sh...]
    reshape x1 -> x0, local copies, waits for them, and re-layouts: 1.31 us -> none  [local_step(): gain2 = gain_vec.reshape(1, model_dim)]
  transfers between devices with their start and end apart: 2 -> 2, of which waited for: 0 -> 0; matrix products, arithmetic and copies ran while one was open for 1% -> 1% of each run, Pallas kernels for 21% -> 23%
where the time goes in v1:
time: 130 us; the launch traced here: 129 us
  Pallas kernels  119 us (92%)
  local copies, waits for them, and re-layouts  5.36 us (4%)
  starting transfers between devices  3.31 us (3%)
    pallas_call x1, Pallas kernels, gather_call(): pl.pallas_call(functools.partial(gather_kernel, group), out_shape=(jax.Sh...  47.4 us
    pallas_call x1, Pallas kernels, finish_call(): pl.pallas_call(functools.partial(finish_kernel, group), out_shape=(jax.Sh...  37.9 us
    pallas_call x1, Pallas kernels, weight_grad_call(): pl.pallas_call(weight_grad_kernel, grid=(model_dim // DW_ROWS, cols // DW...  28.9 us
    pallas_call x1, Pallas kernels, epilogue_call(): pl.pallas_call(epilogue_kernel, out_shape=(jax.ShapeDtypeStruct(u.shape,...  5.04 us
    unnamed x12, local copies, waits for them, and re-layouts  4.56 us
  transfers between devices with their start and end apart: 2, of which 0 were waited for; matrix products, arithmetic and copies ran while one was open for 1% of the time, Pallas kernels for 23%

profile of v1, /device:TPU:112, one launch (start us, length us, event | category | flops | bytes accessed | tf_op | source)
XLA Modules:
  0.0 128.5 jit_solution(7693536188701065265)
XLA Ops:
  0.6 47.4 %gather_dn.1 = (bf16[2,256,3584]{2,1,0:T(8,128)(2,1)}, bf16[2,64,3584]{2,1,0:T(8,128)(2,1)}, f32[2,64,1792]{2,1,0:T(8,128)}, f32[2,64,1792]{2,1,0:T(8,128)}, f32[4,64,1792]{2,1,0:T(8,128)}) custom-call(s32[2,256]{1,0:T(2,128)} %ids_ref.5, bf16[3584]{0:T(1024)(128)(2,1)} %gain_ref.3, bf16[256,3584]{1,0:T(8,128)(2,1)} %table_ref.1, bf16[3584,4608]{1,0:T(8,128)(2,1)} %w_ref.3, ...), custom_call_target="tpu_custom_call" | custom-call | flops 16911433728 | bytes 33030144 | tf_op jit(solution)/shard_map/gather_dn/pallas_call | solution.py:267
  48.0 1.2 collective-permute-start
  49.2 2.1 %collective-permute-start.1 = (f32[2,64,1792]{2,1,0:T(8,128)}, f32[2,64,1792]{2,1,0:T(8,128)}, u32[]{:S(2)}, u32[]{:S(2)}) collective-permute-start(f32[2,64,1792]{2,1,0:T(8,128)} %get-tuple-element.17), channel_id=1, source_target_pairs={{0,6},{1,7},{2,0},{3,1},{4,2},{5,3},{6,4},{7,5},{8,14},{9,15},{10,... | collective-permute-start | bytes 2752520 | tf_op jit(solution)/shard_map/ppermute | solution.py:661
  51.3 0.0 copy-start.1
  51.3 0.0 copy-start.2
  51.3 0.0 copy-start.4
  51.3 28.9 %weight_grad.1 = f32[3584,4608]{1,0:T(8,128)} custom-call(bf16[512,3584]{1,0:T(8,128)(2,1)} %bitcast.2, bf16[512,4608]{1,0:T(8,128)(2,1)} %bitcast.3), custom_call_target="tpu_custom_call" | custom-call | flops 16911433728 | bytes 66060288 | tf_op jit(solution)/shard_map/weight_grad/pallas_call | solution.py:307
  80.3 0.0 copy-done.1
  80.3 0.8 constant_dynamic-slice_fusion
  81.1 0.0 collective-permute-done.rp_ref
  81.1 0.0 collective-permute-done.1.rm_ref
  81.1 0.0 copy-done.2
  81.1 0.0 copy-done.4
  81.1 0.0 copy-start
  81.1 2.0 %copy-done = bf16[2,256,3584]{2,1,0:T(8,128)(2,1)S(1)} copy-done((bf16[2,256,3584]{2,1,0:T(8,128)(2,1)S(1)}, bf16[2,256,3584]{2,1,0:T(8,128)(2,1)}, u32[]{:S(2)}) %copy-start) | copy-done | bytes 3670040
  83.1 0.0 copy-start.3
  83.1 1.0 copy-done.3
  84.1 0.0 copy-start.5
  84.1 1.5 %copy-done.5 = f32[4,64,1792]{2,1,0:T(8,128)S(1)} copy-done((f32[4,64,1792]{2,1,0:T(8,128)S(1)}, f32[4,64,1792]{2,1,0:T(8,128)}, u32[]{:S(2)}) %copy-start.5) | copy-done | bytes 1835032
  85.6 37.9 %finish_u.1 = (bf16[2,256,4608]{2,1,0:T(8,128)(2,1)S(1)}, bf16[2,256,3584]{2,1,0:T(8,128)(2,1)S(1)}, f32[1,3584]{1,0:T(1,128)S(1)}) custom-call(s32[2,256]{1,0:T(2,128)S(1)} %copy-done.2, bf16[3584]{0:T(1024)(128)(2,1)S(1)} %copy-done.4, f32[2,64,1792]{2,1,0:T(8,128)} %collective-permute-done.rp_ref, f32[2,64,1792]{2,1,0:T(8,128)} %collective-permute-done.1.rm_ref, ...), custom_call_target="tpu_custom_call" | custom-call | flops 16911433728 | bytes 33030144 | tf_op jit(solution)/shard_map/finish_u/pallas_call | solution.py:550
  123.5 5.0 %epilogue.1 = (bf16[2,256,4608]{2,1,0:T(8,128)(2,1)}, f32[256,3584]{1,0:T(8,128)}, f32[3584]{0:T(1024)}) custom-call(s32[2,256]{1,0:T(2,128)S(1)} %copy-done.2, bf16[2,256,4608]{2,1,0:T(8,128)(2,1)S(1)} %get-tuple-element.21.u_ref, bf16[2,256,3584]{2,1,0:T(8,128)(2,1)S(1)} %get-tuple-element.22.dx_ref, f32[1,3584]{1,0:T(1,128)S(1)} %get-tuple-element.23.dg_ref), custom_call_target="tpu_custom_call" | custom-call | flops 939524096 | bytes 3670016 | tf_op jit(solution)/shard_map/epilogue/pallas_call | solution.py:628
Async XLA Ops:
  48.0 33.0 %collective-permute-start = (f32[2,64,1792]{2,1,0:T(8,128)}, f32[2,64,1792]{2,1,0:T(8,128)}, u32[]{:S(2)}, u32[]{:S(2)}) collective-permute-start(f32[2,64,1792]{2,1,0:T(8,128)} %get-tuple-element.16), channel_id=1, source_target_pairs={{0,2},{1,3},{2,4},{3,5},{4,6},{5,7},{6,0},{7,1},{8,10},{9,11},{10,... | collective-permute-start | bytes 2752520 | tf_op jit(solution)/shard_map/ppermute | solution.py:660
  49.2 31.8 %collective-permute-start.1 = (f32[2,64,1792]{2,1,0:T(8,128)}, f32[2,64,1792]{2,1,0:T(8,128)}, u32[]{:S(2)}, u32[]{:S(2)}) collective-permute-start(f32[2,64,1792]{2,1,0:T(8,128)} %get-tuple-element.17), channel_id=1, source_target_pairs={{0,6},{1,7},{2,0},{3,1},{4,2},{5,3},{6,4},{7,5},{8,14},{9,15},{10,... | collective-permute-start | bytes 2752520 | tf_op jit(solution)/shard_map/ppermute | solution.py:661
  51.3 28.9 %copy-start.1 = (bf16[2,64,3584]{2,1,0:T(8,128)(2,1)S(1)}, bf16[2,64,3584]{2,1,0:T(8,128)(2,1)}, u32[]{:S(2)}) copy-start(bf16[2,64,3584]{2,1,0:T(8,128)(2,1)} %get-tuple-element.19.xchip_ref) | copy-start | bytes 2752516
  51.3 29.7 %copy-start.2 = (s32[2,256]{1,0:T(2,128)S(1)}, s32[2,256]{1,0:T(2,128)}, u32[]{:S(2)}) copy-start(s32[2,256]{1,0:T(2,128)} %ids_ref.5) | copy-start | bytes 6148
  51.3 29.7 %copy-start.4 = (bf16[3584]{0:T(1024)(128)(2,1)S(1)}, bf16[3584]{0:T(1024)(128)(2,1)}, u32[]{:S(2)}) copy-start(bf16[3584]{0:T(1024)(128)(2,1)} %gain_ref.3) | copy-start | bytes 21508
  81.1 2.0 %copy-start = (bf16[2,256,3584]{2,1,0:T(8,128)(2,1)S(1)}, bf16[2,256,3584]{2,1,0:T(8,128)(2,1)}, u32[]{:S(2)}) copy-start(bf16[2,256,3584]{2,1,0:T(8,128)(2,1)} %get-tuple-element.20.n_ref) | copy-start | bytes 11010052
  83.1 1.0 copy-start.3
  84.1 1.5 %copy-start.5 = (f32[4,64,1792]{2,1,0:T(8,128)S(1)}, f32[4,64,1792]{2,1,0:T(8,128)}, u32[]{:S(2)}) copy-start(f32[4,64,1792]{2,1,0:T(8,128)} %get-tuple-element.18.keep_ref) | copy-start | bytes 5505028

commit v2 on v1

--- a/solution.py
+++ b/solution.py
@@ -14,8 +14,9 @@
 DN_TILE = 256
 RELAY_AT = (3, 5)
 SUM_AT = (10, 12)
-DW_ROWS = 896
-DW_COLS = 1536
+DW_ROWS = 256
+DW_COLS = 2304
+DW_SLOTS = 6
 U_COLS = 256
 U_HOOKS = (5, 7, 10, 12, 17, 15)
 DE_COLS = 512
@@ -296,21 +297,79 @@
     )(ids, gain2, table, w, du)
 
 
-def weight_grad_kernel(n_ref, du_ref, out_ref):
-    cols = pl.ds(pl.multiple_of(pl.program_id(1) * DW_COLS, DW_COLS), DW_COLS)
-    out_ref[...] = lax.dot_general(n_ref[...], du_ref[:, cols], (((0,), (0,)), ((), ())), preferred_element_type=F32)
+def weight_grad_kernel(n_ref, du_ref, out_ref, n_v, du_v, obuf, nsem, dsem, osem):
+    _, model_dim = n_v.shape
+    cols = du_v.shape[1]
+    parts = cols // DW_COLS
+    blocks = model_dim // DW_ROWS
+
+    def at(i, n):
+        return pl.ds(pl.multiple_of(i * n, n), n)
+
+    def du_copy(j):
+        return pltpu.make_async_copy(du_ref.at[:, at(j, DW_COLS)], du_v.at[:, at(j, DW_COLS)], dsem.at[j])
+
+    def n_copy(i):
+        return pltpu.make_async_copy(n_ref.at[:, at(i, DW_ROWS)], n_v.at[:, at(i, DW_ROWS)], nsem.at[i])
+
+    def out_copy(s):
+        i, j = lax.div(s, parts), lax.rem(s, parts)
+        slot = lax.rem(s, DW_SLOTS)
+        return pltpu.make_async_copy(obuf.at[slot], out_ref.at[at(i, DW_ROWS), at(j, DW_COLS)], osem.at[slot])
+
+    n_copy(0).start()
+    for j in range(parts):
+        du_copy(j).start()
+    for i in range(1, blocks):
+        n_copy(i).start()
+
+    def step(s, carry):
+        i, j = lax.div(s, parts), lax.rem(s, parts)
+
+        @pl.when(j == 0)
+        def _():
+            n_copy(i).wait()
+
+        @pl.when(i == 0)
+        def _():
+            du_copy(j).wait()
+
+        @pl.when(s >= DW_SLOTS)
+        def _():
+            out_copy(s - DW_SLOTS).wait()
+
+        obuf[lax.rem(s, DW_SLOTS)] = lax.dot_general(n_v[:, at(i, DW_ROWS)], du_v[:, at(j, DW_COLS)], (((0,), (0,)), ((), ())),
+                                                    preferred_element_type=F32)
+        out_copy(s).start()
+        return carry
+
+    lax.fori_loop(0, blocks * parts, step, 0)
+
+    def drain(s, carry):
+        out_copy(s).wait()
+        return carry
+
+    lax.fori_loop(blocks * parts - DW_SLOTS, blocks * parts, drain, 0)
 
 
 def weight_grad_call(n2, du2):
     total, model_dim = n2.shape
     cols = du2.shape[1]
+    any_spec = pl.BlockSpec(memory_space=pl.ANY)
     return pl.pallas_call(
         weight_grad_kernel,
-        grid=(model_dim // DW_ROWS, cols // DW_COLS),
         out_shape=jax.ShapeDtypeStruct((model_dim, cols), F32),
-        in_specs=[pl.BlockSpec((total, DW_ROWS), lambda i, j: (0, i)), pl.BlockSpec((total, cols), lambda i, j: (0, 0))],
-        out_specs=pl.BlockSpec((DW_ROWS, DW_COLS), lambda i, j: (i, j)),
-        compiler_params=pltpu.CompilerParams(dimension_semantics=("arbitrary", "arbitrary"), vmem_limit_bytes=63 * 1024 * 1024),
+        in_specs=[any_spec, any_spec],
+        out_specs=any_spec,
+        scratch_shapes=[
+            pltpu.VMEM((total, model_dim), BF16),
+            pltpu.VMEM((total, cols), BF16),
+            pltpu.VMEM((DW_SLOTS, DW_ROWS, DW_COLS), F32),
+            pltpu.SemaphoreType.DMA((model_dim // DW_ROWS,)),
+            pltpu.SemaphoreType.DMA((cols // DW_COLS,)),
+            pltpu.SemaphoreType.DMA((DW_SLOTS,)),
+        ],
+        compiler_params=pltpu.CompilerParams(vmem_limit_bytes=63 * 1024 * 1024),
         cost_estimate=pl.CostEstimate(flops=2 * total * cols * model_dim, bytes_accessed=4 * cols * model_dim, transcendentals=0),
         name="weight_grad",
     )(n2, du2)
@@ -582,11 +641,15 @@
         compiler_params=pltpu.CompilerParams(collective_id=1, has_side_effects=True, vmem_limit_bytes=30 * 1024 * 1024),
         cost_estimate=pl.CostEstimate(flops=2 * total * cols_loc * model_dim, bytes_accessed=2 * cols_loc * model_dim, transcendentals=0),
         name="finish_u",
-    )(ids, gain2, rp, rm, keep, xchip, dres, n3, w)
-
-
-def epilogue_kernel(ids_ref, u_ref, dx_ref, dg_ref, u_out, de_out, dg_out, u_v, dx_v, de_v, usem, xsem):
+    )(ids, gain2, *[pltpu.with_memory_space_constraint(v, pltpu.HBM) for v in (rp, rm, keep, xchip, dres, n3, w)])
+
+
+def epilogue_kernel(ids_ref, u_ref, dx_ref, dg_ref, xchip_ref, u_out, de_out, dg_out, x_out, u_v, dx_v, de_v, x_v, usem, xsem, osem):
     dev = lax.axis_index('tp')
+    own_tok = x_v.shape[1]
+    own_rows = pl.ds(pl.multiple_of(lax.rem(dev, 2) * own_tok, own_tok), own_tok)
+    own_in = pltpu.make_async_copy(xchip_ref.at[:, own_rows], x_v, osem.at[0])
+    own_out = pltpu.make_async_copy(x_v, x_out, osem.at[1])
     micro, seq_len = ids_ref.shape
     rows_loc, model_dim = de_v.shape
     steps = model_dim // DE_COLS
@@ -603,6 +666,7 @@
         cp.start()
     for cp in x_loads[2:]:
         cp.start()
+    own_in.start()
     dg_out[...] = dg_ref[0]
     row_id = lax.broadcasted_iota(jnp.int32, (rows_loc, seq_len), 0) + dev * rows_loc
     hot = jnp.concatenate([jnp.where(row_id == ids_ref[m:m + 1, :], 1.0, 0.0).astype(BF16) for m in range(micro)], axis=1)
@@ -615,11 +679,13 @@
         if i < U_PARTS:
             u_loads[i].wait()
             u_stores[i].start()
-    for cp in u_stores + de_stores:
+    own_in.wait()
+    own_out.start()
+    for cp in u_stores + de_stores + [own_out]:
         cp.wait()
 
 
-def epilogue_call(rows_loc, ids, u, dx, dg):
+def epilogue_call(rows_loc, ids, u, dx, dg, xchip):
     micro, seq_len, _ = u.shape
     model_dim = dx.shape[2]
     steps = model_dim // DE_COLS
@@ -628,20 +694,23 @@
     return pl.pallas_call(
         epilogue_kernel,
         out_shape=(jax.ShapeDtypeStruct(u.shape, BF16), jax.ShapeDtypeStruct((rows_loc, model_dim), F32),
-                   jax.ShapeDtypeStruct((model_dim,), F32)),
-        in_specs=[vmem_spec, any_spec, any_spec, vmem_spec],
-        out_specs=(any_spec, any_spec, vmem_spec),
+                   jax.ShapeDtypeStruct((model_dim,), F32),
+                   jax.ShapeDtypeStruct((micro, xchip.shape[1] // 2, model_dim), BF16)),
+        in_specs=[vmem_spec, any_spec, any_spec, vmem_spec, any_spec],
+        out_specs=(any_spec, any_spec, vmem_spec, any_spec),
         scratch_shapes=[
             pltpu.VMEM(u.shape, BF16),
             pltpu.VMEM(dx.shape, BF16),
             pltpu.VMEM((rows_loc, model_dim), F32),
+            pltpu.VMEM((micro, xchip.shape[1] // 2, model_dim), BF16),
             pltpu.SemaphoreType.DMA((2 * U_PARTS,)),
             pltpu.SemaphoreType.DMA((2 * steps,)),
+            pltpu.SemaphoreType.DMA((2,)),
         ],
         compiler_params=pltpu.CompilerParams(vmem_limit_bytes=22 * 1024 * 1024),
         cost_estimate=pl.CostEstimate(flops=2 * micro * seq_len * rows_loc * model_dim, bytes_accessed=4 * rows_loc * model_dim, transcendentals=0),
         name="epilogue",
-    )(ids, u, dx, dg)
+    )(ids, u, dx, dg, xchip)
 
 
 def solution(mesh):
@@ -652,17 +721,14 @@
     def local_step(token_ids, table_loc, gain_vec, w_loc, du_loc, dres_loc):
         micro, seq_len = token_ids.shape
         model_dim, cols_loc = w_loc.shape
-        own_tok = dres_loc.shape[1]
         total = micro * seq_len
-        core = lax.rem(lax.axis_index('tp'), 2)
         gain2 = gain_vec
         normed, x_chip, msg_plus, msg_minus, keep = gather_call(group, token_ids, gain2, table_loc, w_loc, du_loc)
         got_plus = lax.ppermute(msg_plus, 'tp', plus)
         got_minus = lax.ppermute(msg_minus, 'tp', minus)
         grad_w = weight_grad_call(normed.reshape(total, model_dim), du_loc.reshape(total, cols_loc))
         u_tmp, dx_all, dg = finish_call(group, token_ids, gain2, got_plus, got_minus, keep, x_chip, dres_loc, normed, w_loc)
-        u, grad_table, grad_gain = epilogue_call(table_loc.shape[0], token_ids, u_tmp, dx_all, dg)
-        x_own = lax.dynamic_slice_in_dim(x_chip, core * own_tok, own_tok, axis=1)
+        u, grad_table, grad_gain, x_own = epilogue_call(table_loc.shape[0], token_ids, u_tmp, dx_all, dg, x_chip)
         return u, x_own, grad_table, grad_w, grad_gain
 
     return jax.shard_map(local_step, mesh=mesh,

time: 130 us -> 125 us (0.962)
  local copies, waits for them, and re-layouts: 5.36 us -> 0.92 us
    unnamed x12 -> x8, local copies, waits for them, and re-layouts: 4.56 us -> 0.92 us
    pallas_call x1, Pallas kernels: 28.9 us -> 27.6 us  [weight_grad_call(): pl.pallas_call(weight_grad_kernel, out_shape=jax.ShapeDtypeStruct((model_...]
  transfers between devices with their start and end apart: 2 -> 2, of which waited for: 0 -> 0; matrix products, arithmetic and copies ran while one was open for 1% -> 0% of each run, Pallas kernels for 23% -> 22%
where the time goes in v2:
time: 125 us; the launch traced here: 123 us
  Pallas kernels  118 us (94%)
  starting transfers between devices  3.31 us (3%)
    pallas_call x1, Pallas kernels, gather_call(): pl.pallas_call(functools.partial(gather_kernel, group), out_shape=(jax.Sh...  47.4 us
    pallas_call x1, Pallas kernels, finish_call(): pl.pallas_call(functools.partial(finish_kernel, group), out_shape=(jax.Sh...  38.2 us
    pallas_call x1, Pallas kernels, weight_grad_call(): pl.pallas_call(weight_grad_kernel, out_shape=jax.ShapeDtypeStruct((model_...  27.6 us
    pallas_call x1, Pallas kernels, epilogue_call(): pl.pallas_call(epilogue_kernel, out_shape=(jax.ShapeDtypeStruct(u.shape,...  5.34 us
  transfers between devices with their start and end apart: 2, of which 0 were waited for; matrix products, arithmetic and copies ran while one was open for 0% of the time, Pallas kernels for 22%

profile of v2, /device:TPU:112, one launch (start us, length us, event | category | flops | bytes accessed | tf_op | source)
XLA Modules:
  0.0 123.4 jit_solution(17812069930973223176)
XLA Ops:
  0.6 47.4 %gather_dn.1 = (bf16[2,256,3584]{2,1,0:T(8,128)(2,1)}, bf16[2,64,3584]{2,1,0:T(8,128)(2,1)}, f32[2,64,1792]{2,1,0:T(8,128)}, f32[2,64,1792]{2,1,0:T(8,128)}, f32[4,64,1792]{2,1,0:T(8,128)}) custom-call(s32[2,256]{1,0:T(2,128)} %ids_ref.5, bf16[3584]{0:T(1024)(128)(2,1)} %gain_ref.3, bf16[256,3584]{1,0:T(8,128)(2,1)} %table_ref.1, bf16[3584,4608]{1,0:T(8,128)(2,1)} %w_ref.3, ...), custom_call_target="tpu_custom_call" | custom-call | flops 16911433728 | bytes 33030144 | tf_op jit(solution)/shard_map/gather_dn/pallas_call | solution.py:268
  48.0 1.2 collective-permute-start
  49.2 2.1 %collective-permute-start.1 = (f32[2,64,1792]{2,1,0:T(8,128)}, f32[2,64,1792]{2,1,0:T(8,128)}, u32[]{:S(2)}, u32[]{:S(2)}) collective-permute-start(f32[2,64,1792]{2,1,0:T(8,128)} %get-tuple-element.18), channel_id=1, source_target_pairs={{0,6},{1,7},{2,0},{3,1},{4,2},{5,3},{6,4},{7,5},{8,14},{9,15},{10,... | collective-permute-start | bytes 2752520 | tf_op jit(solution)/shard_map/ppermute | solution.py:728
  51.3 0.0 copy-start.1
  51.3 0.0 copy-start.2
  51.3 27.6 %weight_grad.1 = f32[3584,4608]{1,0:T(8,128)} custom-call(bf16[512,3584]{1,0:T(8,128)(2,1)} %bitcast.3, bf16[512,4608]{1,0:T(8,128)(2,1)} %bitcast.2), custom_call_target="tpu_custom_call" | custom-call | flops 16911433728 | bytes 66060288 | tf_op jit(solution)/shard_map/weight_grad/pallas_call | solution.py:359
  78.9 0.0 collective-permute-done.rp_ref
  78.9 0.0 copy-start.3
  79.0 0.0 collective-permute-done.1.rm_ref
  79.0 0.9 copy-done.3
  79.9 0.0 copy-done.1
  79.9 0.0 copy-done.2
  79.9 0.0 copy-start
  79.9 38.2 %finish_u.1 = (bf16[2,256,4608]{2,1,0:T(8,128)(2,1)S(1)}, bf16[2,256,3584]{2,1,0:T(8,128)(2,1)S(1)}, f32[1,3584]{1,0:T(1,128)S(1)}) custom-call(s32[2,256]{1,0:T(2,128)S(1)} %copy-done.1, bf16[3584]{0:T(1024)(128)(2,1)S(1)} %copy-done.2, f32[2,64,1792]{2,1,0:T(8,128)} %copy-done.3, f32[2,64,1792]{2,1,0:T(8,128)} %collective-permute-done.1.rm_ref, ...), custom_call_target="tpu_custom_call" | custom-call | flops 16911433728 | bytes 33030144 | tf_op jit(solution)/shard_map/finish_u/pallas_call | solution.py:609
  118.1 0.0 copy-done
  118.1 5.3 %epilogue.1 = (bf16[2,256,4608]{2,1,0:T(8,128)(2,1)}, f32[256,3584]{1,0:T(8,128)}, f32[3584]{0:T(1024)}, bf16[2,32,3584]{2,1,0:T(8,128)(2,1)}) custom-call(s32[2,256]{1,0:T(2,128)S(1)} %copy-done.1, bf16[2,256,4608]{2,1,0:T(8,128)(2,1)S(1)} %get-tuple-element.22.u_ref, bf16[2,256,3584]{2,1,0:T(8,128)(2,1)S(1)} %get-tuple-element.23.dx_ref, ...), custom_call_target="tpu_custom_call" | custom-call | flops 939524096 | bytes 3670016 | tf_op jit(solution)/shard_map/epilogue/pallas_call | solution.py:694
Async XLA Ops:
  48.0 30.9 %collective-permute-start = (f32[2,64,1792]{2,1,0:T(8,128)}, f32[2,64,1792]{2,1,0:T(8,128)S(1)}, u32[]{:S(2)}, u32[]{:S(2)}) collective-permute-start(f32[2,64,1792]{2,1,0:T(8,128)} %get-tuple-element.17), channel_id=1, source_target_pairs={{0,2},{1,3},{2,4},{3,5},{4,6},{5,7},{6,0},{7,1},{8,10},{9,11},{10,... | collective-permute-start | bytes 2752520 | tf_op jit(solution)/shard_map/ppermute | solution.py:727
  49.2 29.7 %collective-permute-start.1 = (f32[2,64,1792]{2,1,0:T(8,128)}, f32[2,64,1792]{2,1,0:T(8,128)}, u32[]{:S(2)}, u32[]{:S(2)}) collective-permute-start(f32[2,64,1792]{2,1,0:T(8,128)} %get-tuple-element.18), channel_id=1, source_target_pairs={{0,6},{1,7},{2,0},{3,1},{4,2},{5,3},{6,4},{7,5},{8,14},{9,15},{10,... | collective-permute-start | bytes 2752520 | tf_op jit(solution)/shard_map/ppermute | solution.py:728
  51.3 28.5 %copy-start.1 = (s32[2,256]{1,0:T(2,128)S(1)}, s32[2,256]{1,0:T(2,128)}, u32[]{:S(2)}) copy-start(s32[2,256]{1,0:T(2,128)} %ids_ref.5) | copy-start | bytes 6148
  51.3 28.5 %copy-start.2 = (bf16[3584]{0:T(1024)(128)(2,1)S(1)}, bf16[3584]{0:T(1024)(128)(2,1)}, u32[]{:S(2)}) copy-start(bf16[3584]{0:T(1024)(128)(2,1)} %gain_ref.3) | copy-start | bytes 21508
  78.9 0.9 copy-start.3
  79.9 38.2 %copy-start = (bf16[2,64,3584]{2,1,0:T(8,128)(2,1)S(1)}, bf16[2,64,3584]{2,1,0:T(8,128)(2,1)}, u32[]{:S(2)}) copy-start(bf16[2,64,3584]{2,1,0:T(8,128)(2,1)} %get-tuple-element.20.xchip_ref) | copy-start | bytes 2752516

commit v3 on v2

--- a/solution.py
+++ b/solution.py
@@ -12,20 +12,19 @@
 F32 = jnp.float32
 BF16 = jnp.bfloat16
 DN_TILE = 256
-RELAY_AT = (3, 5)
-SUM_AT = (10, 12)
+RELAY_AT = (2, 4)
+SUM_AT = (9, 10)
 DW_ROWS = 256
 DW_COLS = 2304
-DW_SLOTS = 6
 U_COLS = 256
-U_HOOKS = (5, 7, 10, 12, 17, 15)
+U_HOOKS = (3, 4, 6, 7, 9, 11, 13, 15)
 DE_COLS = 512
 U_PARTS = 4
 
 
 def gather_kernel(group, ids_ref, gain_ref, table_ref, w_ref, du_ref,
                   n_out, xchip_out, plus_out, minus_out, keep_out,
-                  tab, looked, r_relay, r_direct, r_comb, s_comb, xbuf, n_v, du_v, wbuf, dn2, dnp, stage,
+                  tab, hot, looked, r_relay, r_direct, r_comb, s_comb, xbuf, n_v, du_v, wbuf, dn2, dnp, stage,
                   lsem, wsem, osem, snd, rcv):
     dev = lax.axis_index('tp')
     chips = group // 2
@@ -106,12 +105,13 @@
         cols = pl.ds(pl.multiple_of(t * DN_TILE, DN_TILE), DN_TILE)
         return remote(dn2.at[0, :, :, cols], dnp.at[:, :, cols], 31 + t, partner)
 
+    row_id = lax.broadcasted_iota(jnp.int32, (2 * rows_loc, seq_len), 0) + chip * (2 * rows_loc)
+    for m in range(micro):
+        hot[m] = jnp.where(row_id == ids_ref[m:m + 1, :], 1.0, 0.0).astype(BF16).T
     cp_tab.wait()
     table_msg.wait_recv()
-    row_id = lax.broadcasted_iota(jnp.int32, (2 * rows_loc, seq_len), 0) + chip * (2 * rows_loc)
-    for m in (1, 0):
-        hot = jnp.where(row_id == ids_ref[m:m + 1, :], 1.0, 0.0).astype(BF16)
-        looked[m] = lax.dot_general(hot, tab[...], (((0,), (0,)), ((), ())), preferred_element_type=F32).astype(BF16)
+    for m in range(micro):
+        looked[m] = jnp.dot(hot[m], tab[...], preferred_element_type=F32).astype(BF16)
     for q in range(2):
         for m in range(2):
             relay(m, q).start()
@@ -163,11 +163,6 @@
 
     lax.fori_loop(0, 2 * tiles, dn_step, 0)
 
-    def dn_wait(t, carry):
-        dn_msg(t).wait_recv()
-        return carry
-
-    lax.fori_loop(0, tiles, dn_wait, 0)
 
     terms = ((2, 1), (1, 0), (2, 0), (3, 1), (1, 1), (3, 0), (0, 0), (0, 1))
 
@@ -188,7 +183,12 @@
         far(q, 1).start()
         near_fwd(q, 1).start()
 
+    def dn_wait(t, carry):
+        dn_msg(t).wait_recv()
+        return carry
+
     near_step(0)
+    lax.fori_loop(0, tiles, dn_wait, 0)
     s_steps()
     near_step(1)
 
@@ -276,6 +276,7 @@
         out_specs=(hbm_spec,) * 5,
         scratch_shapes=[
             pltpu.VMEM((2 * rows_loc, half), BF16),
+            pltpu.VMEM((micro, seq_len, 2 * rows_loc), BF16),
             pltpu.VMEM((micro, seq_len, half), BF16),
             msg, msg, msg, msg,
             pltpu.VMEM((micro, seq_len, model_dim), BF16),
@@ -297,7 +298,7 @@
     )(ids, gain2, table, w, du)
 
 
-def weight_grad_kernel(n_ref, du_ref, out_ref, n_v, du_v, obuf, nsem, dsem, osem):
+def weight_grad_kernel(n_ref, du_ref, out_ref, n_v, du_v, even, odd, obuf, nsem, dsem, osem):
     _, model_dim = n_v.shape
     cols = du_v.shape[1]
     parts = cols // DW_COLS
@@ -312,9 +313,8 @@
     def n_copy(i):
         return pltpu.make_async_copy(n_ref.at[:, at(i, DW_ROWS)], n_v.at[:, at(i, DW_ROWS)], nsem.at[i])
 
-    def out_copy(s):
+    def out_copy(s, slot):
         i, j = lax.div(s, parts), lax.rem(s, parts)
-        slot = lax.rem(s, DW_SLOTS)
         return pltpu.make_async_copy(obuf.at[slot], out_ref.at[at(i, DW_ROWS), at(j, DW_COLS)], osem.at[slot])
 
     n_copy(0).start()
@@ -322,34 +322,40 @@
         du_copy(j).start()
     for i in range(1, blocks):
         n_copy(i).start()
-
-    def step(s, carry):
-        i, j = lax.div(s, parts), lax.rem(s, parts)
-
-        @pl.when(j == 0)
-        def _():
-            n_copy(i).wait()
-
-        @pl.when(i == 0)
-        def _():
-            du_copy(j).wait()
-
-        @pl.when(s >= DW_SLOTS)
-        def _():
-            out_copy(s - DW_SLOTS).wait()
-
-        obuf[lax.rem(s, DW_SLOTS)] = lax.dot_general(n_v[:, at(i, DW_ROWS)], du_v[:, at(j, DW_COLS)], (((0,), (0,)), ((), ())),
-                                                    preferred_element_type=F32)
-        out_copy(s).start()
+    n_copy(0).wait()
+    even[...] = n_v[:, at(0, DW_ROWS)].T
+
+    def pair(p, carry):
+        for e in range(2):
+            i = 2 * p + e
+            here, there = (even, odd) if e == 0 else (odd, even)
+            nxt = jnp.minimum(i + 1, blocks - 1)
+
+            @pl.when(i + 1 < blocks)
+            def _():
+                n_copy(i + 1).wait()
+
+            for j in range(parts):
+                slot = e * parts + j
+
+                @pl.when(i == 0)
+                def _():
+                    du_copy(j).wait()
+
+                @pl.when(p > 0)
+                def _():
+                    out_copy((i - 2) * parts + j, slot).wait()
+            there[...] = n_v[:, at(nxt, DW_ROWS)].T
+            for j in range(parts):
+                slot = e * parts + j
+                obuf[slot] = jnp.dot(here[...], du_v[:, j * DW_COLS:(j + 1) * DW_COLS], preferred_element_type=F32)
+                out_copy(i * parts + j, slot).start()
         return carry
 
-    lax.fori_loop(0, blocks * parts, step, 0)
-
-    def drain(s, carry):
-        out_copy(s).wait()
-        return carry
-
-    lax.fori_loop(blocks * parts - DW_SLOTS, blocks * parts, drain, 0)
+    lax.fori_loop(0, blocks // 2, pair, 0)
+    for e in range(2):
+        for j in range(parts):
+            out_copy((blocks - 2 + e) * parts + j, e * parts + j).wait()
 
 
 def weight_grad_call(n2, du2):
@@ -364,20 +370,22 @@
         scratch_shapes=[
             pltpu.VMEM((total, model_dim), BF16),
             pltpu.VMEM((total, cols), BF16),
-            pltpu.VMEM((DW_SLOTS, DW_ROWS, DW_COLS), F32),
+            pltpu.VMEM((DW_ROWS, total), BF16),
+            pltpu.VMEM((DW_ROWS, total), BF16),
+            pltpu.VMEM((2 * cols // DW_COLS, DW_ROWS, DW_COLS), F32),
             pltpu.SemaphoreType.DMA((model_dim // DW_ROWS,)),
             pltpu.SemaphoreType.DMA((cols // DW_COLS,)),
-            pltpu.SemaphoreType.DMA((DW_SLOTS,)),
+            pltpu.SemaphoreType.DMA((2 * cols // DW_COLS,)),
         ],
-        compiler_params=pltpu.CompilerParams(vmem_limit_bytes=63 * 1024 * 1024),
+        compiler_params=pltpu.CompilerParams(vmem_limit_bytes=67043328),
         cost_estimate=pl.CostEstimate(flops=2 * total * cols * model_dim, bytes_accessed=4 * cols * model_dim, transcendentals=0),
         name="weight_grad",
     )(n2, du2)
 
 
-def finish_kernel(group, ids_ref, gain_ref, rp_ref, rm_ref, keep_ref, xchip_ref, dres_ref, n_ref, w_ref,
+def finish_kernel(group, gain_hbm, rp_ref, rm_ref, keep_ref, xchip_ref, dres_ref, n_ref, w_ref,
                   u_out, dx_out, dg_out,
-                  rp, rm, keep, xc, dres, n_v, wbuf, ubuf, s_comb, r_comb, dn_v, dot_s, dot_r, dxbuf, dg_v, dg_r, dg_half,
+                  gain_ref, rp, rm, keep, xc, dres, n_v, wbuf, ubuf, s_comb, r_comb, dn_v, dot_s, dot_r, dxbuf, dg_v, dg_r, dg_half,
                   lsem, wsem, usem, osem, snd, rcv):
     dev = lax.axis_index('tp')
     chips = group // 2
@@ -387,8 +395,7 @@
     minus = lax.rem(dev + group - 2, group)
     opposite = lax.rem(dev + group // 2, group)
     partner = dev + 1 - 2 * core
-    micro, seq_len = ids_ref.shape
-    model_dim = gain_ref.shape[0]
+    micro, seq_len, model_dim = n_ref.shape
     half = model_dim // 2
     ctok = seq_len // chips
     qrows = ctok // 2
@@ -415,7 +422,7 @@
 
     own_rows = pl.ds(pl.multiple_of(core * qrows, qrows), qrows)
     loads = [local(rp_ref, rp, 0), local(rm_ref, rm, 1), local(keep_ref, keep, 2), local(xchip_ref, xc, 3),
-             local(n_ref, n_v, 4), local(dres_ref.at[:, :, my_cols], dres.at[:, own_rows], 5)]
+             local(n_ref, n_v, 4), local(dres_ref.at[:, :, my_cols], dres.at[:, own_rows], 5), local(gain_hbm, gain_ref, 6)]
     for cp in loads[:4]:
         cp.start()
 
@@ -429,6 +436,7 @@
 
     loads[4].start()
     loads[5].start()
+    loads[6].start()
     w_copy(0).start()
 
     barrier = pltpu.get_barrier_semaphore()
@@ -524,6 +532,11 @@
         far(q, 1).start()
         near_fwd(q, 1).start()
 
+    def far_step(q):
+        for m in range(2):
+            far(q, m).wait_recv()
+            far_fwd(q, m).start()
+
     def dg_step():
         for way in range(3):
             dg_msg(way).wait_recv()
@@ -531,7 +544,8 @@
         dg_fin.start()
 
     hooks = ((U_HOOKS[0], lambda: dn_finish(0)), (U_HOOKS[1], lambda: dx_finish(0)), (U_HOOKS[2], lambda: dn_finish(1)),
-             (U_HOOKS[3], lambda: dx_finish(1)), (U_HOOKS[4], lambda: near_step(0)), (U_HOOKS[5], dg_step))
+             (U_HOOKS[3], lambda: dx_finish(1)), (U_HOOKS[4], lambda: near_step(0)), (U_HOOKS[5], dg_step),
+             (U_HOOKS[6], lambda: near_step(1)), (U_HOOKS[7], lambda: far_step(0)))
 
     def u_step(t, carry):
         @pl.when(t + 1 < steps)
@@ -552,11 +566,7 @@
         return carry
 
     lax.fori_loop(0, steps, u_step, 0)
-    near_step(1)
-    for q in range(2):
-        for m in range(2):
-            far(q, m).wait_recv()
-            far_fwd(q, m).start()
+    far_step(1)
     dg_fin.wait_recv()
     dg_copies = [pltpu.make_async_copy(dg_half.at[0], dg_out.at[:, my_cols], osem.at[0]),
                  pltpu.make_async_copy(dg_half.at[1], dg_out.at[:, his_cols], osem.at[1])]
@@ -595,8 +605,8 @@
             spread(q, way).wait_send()
 
 
-def finish_call(group, ids, gain2, rp, rm, keep, xchip, dres, n3, w):
-    micro, seq_len = ids.shape
+def finish_call(group, gain2, rp, rm, keep, xchip, dres, n3, w):
+    micro, seq_len, _ = n3.shape
     model_dim, cols_loc = w.shape
     half = model_dim // 2
     chips = group // 2
@@ -605,15 +615,15 @@
     total = micro * seq_len
     hbm_spec = pl.BlockSpec(memory_space=pltpu.HBM)
     any_spec = pl.BlockSpec(memory_space=pl.ANY)
-    vmem_spec = pl.BlockSpec(memory_space=pltpu.VMEM)
     return pl.pallas_call(
         functools.partial(finish_kernel, group),
         out_shape=(jax.ShapeDtypeStruct((micro, seq_len, cols_loc), BF16),
                    jax.ShapeDtypeStruct((micro, seq_len, model_dim), BF16),
                    jax.ShapeDtypeStruct((1, model_dim), F32)),
-        in_specs=[vmem_spec, vmem_spec] + [hbm_spec] * 7,
+        in_specs=[hbm_spec] * 8,
         out_specs=(any_spec,) * 3,
         scratch_shapes=[
+            pltpu.VMEM((model_dim,), BF16),
             pltpu.VMEM((2, ctok, half), F32),
             pltpu.VMEM((2, ctok, half), F32),
             pltpu.VMEM((4, ctok, half), F32),
@@ -631,7 +641,7 @@
             pltpu.VMEM((1, half), F32),
             pltpu.VMEM((3, 1, half), F32),
             pltpu.VMEM((2, 1, half), F32),
-            pltpu.SemaphoreType.DMA((6,)),
+            pltpu.SemaphoreType.DMA((7,)),
             pltpu.SemaphoreType.DMA((2,)),
             pltpu.SemaphoreType.DMA((2,)),
             pltpu.SemaphoreType.DMA((2 + chips,)),
@@ -641,7 +651,7 @@
         compiler_params=pltpu.CompilerParams(collective_id=1, has_side_effects=True, vmem_limit_bytes=30 * 1024 * 1024),
         cost_estimate=pl.CostEstimate(flops=2 * total * cols_loc * model_dim, bytes_accessed=2 * cols_loc * model_dim, transcendentals=0),
         name="finish_u",
-    )(ids, gain2, *[pltpu.with_memory_space_constraint(v, pltpu.HBM) for v in (rp, rm, keep, xchip, dres, n3, w)])
+    )(*[pltpu.with_memory_space_constraint(v, pltpu.HBM) for v in (gain2, rp, rm, keep, xchip, dres, n3, w)])
 
 
 def epilogue_kernel(ids_ref, u_ref, dx_ref, dg_ref, xchip_ref, u_out, de_out, dg_out, x_out, u_v, dx_v, de_v, x_v, usem, xsem, osem):
@@ -727,7 +737,7 @@
         got_plus = lax.ppermute(msg_plus, 'tp', plus)
         got_minus = lax.ppermute(msg_minus, 'tp', minus)
         grad_w = weight_grad_call(normed.reshape(total, model_dim), du_loc.reshape(total, cols_loc))
-        u_tmp, dx_all, dg = finish_call(group, token_ids, gain2, got_plus, got_minus, keep, x_chip, dres_loc, normed, w_loc)
+        u_tmp, dx_all, dg = finish_call(group, gain2, got_plus, got_minus, keep, x_chip, dres_loc, normed, w_loc)
         u, grad_table, grad_gain, x_own = epilogue_call(table_loc.shape[0], token_ids, u_tmp, dx_all, dg, x_chip)
         return u, x_own, grad_table, grad_w, grad_gain
 

time: 125 us -> 118 us (0.944)
  Pallas kernels: 118 us -> 113 us
    pallas_call x1, Pallas kernels: 38.2 us -> 34.5 us  [finish_call(): pl.pallas_call(functools.partial(finish_kernel, group), out_shape=(jax.Sh...]
    pallas_call x1, Pallas kernels: 27.6 us -> 25.9 us  [weight_grad_call(): pl.pallas_call(weight_grad_kernel, out_shape=jax.ShapeDtypeStruct((model_...]
where the time goes in v3:
time: 118 us; the launch traced here: 117 us
  Pallas kernels  113 us (96%)
  starting transfers between devices  3.31 us (3%)
    pallas_call x1, Pallas kernels, gather_call(): pl.pallas_call(functools.partial(gather_kernel, group), out_shape=(jax.Sh...  47 us
    pallas_call x1, Pallas kernels, finish_call(): pl.pallas_call(functools.partial(finish_kernel, group), out_shape=(jax.Sh...  34.5 us
    pallas_call x1, Pallas kernels, weight_grad_call(): pl.pallas_call(weight_grad_kernel, out_shape=jax.ShapeDtypeStruct((model_...  25.9 us
    pallas_call x1, Pallas kernels, epilogue_call(): pl.pallas_call(epilogue_kernel, out_shape=(jax.ShapeDtypeStruct(u.shape,...  5.34 us
    ppermute x1, starting transfers between devices, local_step(): got_minus = lax.ppermute(msg_minus, 'tp', minus)  2.93 us
  transfers between devices with their start and end apart: 2, of which 0 were waited for; matrix products, arithmetic and copies ran while one was open for 0% of the time, Pallas kernels for 22%

profile of v3, /device:TPU:112, one launch (start us, length us, event | category | flops | bytes accessed | tf_op | source)
XLA Modules:
  0.0 116.8 jit_solution(1674477080282552900)
XLA Ops:
  0.6 47.0 %gather_dn.1 = (bf16[2,256,3584]{2,1,0:T(8,128)(2,1)}, bf16[2,64,3584]{2,1,0:T(8,128)(2,1)}, f32[2,64,1792]{2,1,0:T(8,128)}, f32[2,64,1792]{2,1,0:T(8,128)}, f32[4,64,1792]{2,1,0:T(8,128)}) custom-call(s32[2,256]{1,0:T(2,128)} %ids_ref.3, bf16[3584]{0:T(1024)(128)(2,1)} %gain_hbm.1, bf16[256,3584]{1,0:T(8,128)(2,1)} %table_ref.1, bf16[3584,4608]{1,0:T(8,128)(2,1)} %w_ref.3, ...), custom_call_target="tpu_custom_call" | custom-call | flops 16911433728 | bytes 33030144 | tf_op jit(solution)/shard_map/gather_dn/pallas_call | solution.py:268
  47.6 0.4 collective-permute-start
  48.0 2.9 %collective-permute-start.1 = (f32[2,64,1792]{2,1,0:T(8,128)}, f32[2,64,1792]{2,1,0:T(8,128)}, u32[]{:S(2)}, u32[]{:S(2)}) collective-permute-start(f32[2,64,1792]{2,1,0:T(8,128)} %get-tuple-element.18), channel_id=1, source_target_pairs={{0,6},{1,7},{2,0},{3,1},{4,2},{5,3},{6,4},{7,5},{8,14},{9,15},{10,... | collective-permute-start | bytes 2752520 | tf_op jit(solution)/shard_map/ppermute | solution.py:738
  50.9 25.9 %weight_grad.1 = f32[3584,4608]{1,0:T(8,128)} custom-call(bf16[512,3584]{1,0:T(8,128)(2,1)} %bitcast.3, bf16[512,4608]{1,0:T(8,128)(2,1)} %bitcast.2), custom_call_target="tpu_custom_call" | custom-call | flops 16911433728 | bytes 66060288 | tf_op jit(solution)/shard_map/weight_grad/pallas_call | solution.py:365
  76.8 0.0 collective-permute-done.rp_ref
  76.8 0.0 collective-permute-done.1.rm_ref
  76.9 0.0 copy-start
  76.9 0.0 copy-start.1
  76.9 34.5 %finish_u.1 = (bf16[2,256,4608]{2,1,0:T(8,128)(2,1)S(1)}, bf16[2,256,3584]{2,1,0:T(8,128)(2,1)S(1)}, f32[1,3584]{1,0:T(1,128)S(1)}) custom-call(bf16[3584]{0:T(1024)(128)(2,1)} %gain_hbm.1, f32[2,64,1792]{2,1,0:T(8,128)} %collective-permute-done.rp_ref, f32[2,64,1792]{2,1,0:T(8,128)} %collective-permute-done.1.rm_ref, ...), custom_call_target="tpu_custom_call" | custom-call | flops 16911433728 | bytes 33030144 | tf_op jit(solution)/shard_map/finish_u/pallas_call | solution.py:618
  111.4 0.0 copy-done
  111.4 0.0 copy-done.1
  111.5 5.3 %epilogue.1 = (bf16[2,256,4608]{2,1,0:T(8,128)(2,1)}, f32[256,3584]{1,0:T(8,128)}, f32[3584]{0:T(1024)}, bf16[2,32,3584]{2,1,0:T(8,128)(2,1)}) custom-call(s32[2,256]{1,0:T(2,128)S(1)} %copy-done.1, bf16[2,256,4608]{2,1,0:T(8,128)(2,1)S(1)} %get-tuple-element.22.u_ref, bf16[2,256,3584]{2,1,0:T(8,128)(2,1)S(1)} %get-tuple-element.23.dx_ref, ...), custom_call_target="tpu_custom_call" | custom-call | flops 939524096 | bytes 3670016 | tf_op jit(solution)/shard_map/epilogue/pallas_call | solution.py:704
Async XLA Ops:
  47.6 29.2 %collective-permute-start = (f32[2,64,1792]{2,1,0:T(8,128)}, f32[2,64,1792]{2,1,0:T(8,128)}, u32[]{:S(2)}, u32[]{:S(2)}) collective-permute-start(f32[2,64,1792]{2,1,0:T(8,128)} %get-tuple-element.17), channel_id=1, source_target_pairs={{0,2},{1,3},{2,4},{3,5},{4,6},{5,7},{6,0},{7,1},{8,10},{9,11},{10,... | collective-permute-start | bytes 2752520 | tf_op jit(solution)/shard_map/ppermute | solution.py:737
  48.0 28.9 %collective-permute-start.1 = (f32[2,64,1792]{2,1,0:T(8,128)}, f32[2,64,1792]{2,1,0:T(8,128)}, u32[]{:S(2)}, u32[]{:S(2)}) collective-permute-start(f32[2,64,1792]{2,1,0:T(8,128)} %get-tuple-element.18), channel_id=1, source_target_pairs={{0,6},{1,7},{2,0},{3,1},{4,2},{5,3},{6,4},{7,5},{8,14},{9,15},{10,... | collective-permute-start | bytes 2752520 | tf_op jit(solution)/shard_map/ppermute | solution.py:738
  76.9 34.6 %copy-start = (bf16[2,64,3584]{2,1,0:T(8,128)(2,1)S(1)}, bf16[2,64,3584]{2,1,0:T(8,128)(2,1)}, u32[]{:S(2)}) copy-start(bf16[2,64,3584]{2,1,0:T(8,128)(2,1)} %get-tuple-element.20.xchip_ref) | copy-start | bytes 2752516
  76.9 34.6 %copy-start.1 = (s32[2,256]{1,0:T(2,128)S(1)}, s32[2,256]{1,0:T(2,128)}, u32[]{:S(2)}) copy-start(s32[2,256]{1,0:T(2,128)} %ids_ref.3) | copy-start | bytes 6148
